TPU v7x, 32 devices: a whole 2x2x4 slice. The times are simulated.
32 devices in a mesh: gx: 4 (over z), gy: 4 (over x, core), col: 2 (over y).
Axes of the slice: x: 2, y: 2, z: 4, core: 2. Of those that a mesh axis runs over, the one named last changes fastest.
Arguments:
- fields: bfloat16 [2, 128, 128, 32, 128], P('col', 'gx', 'gy'), may hold values from -6 to 6
- spectral: bfloat16 [1, 16, 16, 2, 32, 32, 16], P(None, 'gx', 'gy', None, None, 'col'), may hold values from -0.75 to 0.75
- skip_weight: bfloat16 [1, 32, 32], replicated, may hold values from -1 to 1
- skip_bias: float32 [1, 32], replicated, may hold values from -3 to 3
- norm_gain: float32 [1, 32], replicated, may hold values from 0.5 to 1.5
- norm_shift: float32 [1, 32], replicated, may hold values from -3 to 3
Outputs:
- activations: bfloat16 [2, 128, 128, 32, 128], P('col', 'gx', 'gy')
All inputs are finite; a program needn't handle non-finite values.
Results may differ from a plain program's by a relative error of at most 0.012.
Values may be sent and summed in bfloat16 or wider, within the bound.
A program may use at most 128 MiB of HBM per device.

v0:
```python
import functools
import math

import jax
import jax.numpy as jnp
import numpy as np
from jax import lax
from jax.experimental import pallas as pl
from jax.experimental.pallas import tpu as pltpu
from jax.sharding import PartitionSpec as P

norm_eps = 1e-05
BF = jnp.bfloat16
F32 = jnp.float32
MESH = pl.DeviceIdType.MESH


def signed(count):
    index = np.arange(count)
    return np.where(index < count // 2, index, index - count)


def cos_sin(positions, frequency, length):
    turns = (positions[:, None] * frequency[None, :]) % length
    phase = turns * (2.0 * math.pi / length)
    return np.cos(phase), np.sin(phase)


def log2(n):
    assert n & (n - 1) == 0
    return n.bit_length() - 1


def div(i, n):
    return lax.shift_right_logical(i, jnp.int32(log2(n)))


def mod(i, n):
    return lax.bitwise_and(i, jnp.int32(n - 1))


def iota(shape, dim):
    return lax.broadcasted_iota(jnp.int32, shape, dim)


def dot(a, b):
    return jnp.dot(a, b, preferred_element_type=F32)


def expand(table, rows, cols, row_of, col_of, row_key, col_key, first_row=0):
    r, c = table.shape
    left = (row_of(iota((rows, r), 0) + first_row) == iota((rows, r), 1)).astype(F32).astype(BF)
    right = (col_of(iota((c, cols), 1)) == iota((c, cols), 0)).astype(F32).astype(BF)
    full = dot(dot(left, table).astype(BF), right)
    keep = row_key(iota((rows, cols), 0) + first_row) == col_key(iota((rows, cols), 1))
    return jnp.where(keep, full, 0.0).astype(BF)


def kron_eye(table, n, store, chunk=256):
    rows, cols = table.shape[0] * n, table.shape[1] * n
    chunk = min(chunk, rows)
    for first in range(0, rows, chunk):
        store(
            first,
            expand(
                table, chunk, cols,
                lambda i: div(i, n), lambda j: div(j, n),
                lambda i: mod(i, n), lambda j: mod(j, n), first,
            ),
        )


def front_kernel(
    sizes,
    fields_ref, spectral_ref, depth_ref, tyf_ref, txf_ref, txi_ref, tyi_ref,
    out_ref,
    ky_ref, kx_ref, total_ref, send_ref, recv_ref, mix_ref, modes_ref, gx_ref, hy_ref,
    cm_ref, w_ref, wa_ref,
    wsem, send1, recv1, send2, recv2, send3, recv3,
):
    n_gx, n_gy, n_col, xl, yl, C, MY, MZ, kxl, kyl, dl, G, steps, halves = sizes
    nxy, N = n_gx * n_gy, n_gx * n_gy * n_col
    L = 2 * kxl * MZ
    CH = C // halves
    per = n_col // halves
    half, step = pl.program_id(0), pl.program_id(1)
    gx, gy, col = lax.axis_index("gx"), lax.axis_index("gy"), lax.axis_index("col")

    unrolled = N <= 64
    at_gx = [lax.rem(gx + a, n_gx) for a in range(n_gx)] if unrolled else None
    at_gy = [lax.rem(gy + a, n_gy) for a in range(n_gy)] if unrolled else None
    at_col = [lax.rem(col + a, n_col) for a in range(n_col)] if unrolled else None

    def target(i):
        a, b, c = i // (n_gy * n_col), (i // n_col) % n_gy, i % n_col
        if unrolled:
            return at_gx[a], at_gy[b], at_col[c]
        return (gx + a) % n_gx, (gy + b) % n_gy, (col + c) % n_col

    def loop(low, high, body):
        if unrolled:
            for i in range(low, high):
                body(i)
            return

        def go(i, carry):
            body(i)
            return carry
        lax.fori_loop(low, high, go, 0)

    weights_copy = pltpu.make_async_copy(spectral_ref, w_ref, wsem)

    @pl.when((half == 0) & (step == 0))
    def _():
        barrier = pltpu.get_barrier_semaphore()

        def greet(i):
            px, py, pc = target(i)
            pl.semaphore_signal(
                barrier, inc=1, device_id={"gx": px, "gy": py, "col": pc}, device_id_type=MESH
            )

        loop(1, nxy, lambda i: greet(i * n_col))
        loop(1, n_col, greet)
        weights_copy.start()

        def put(first, value):
            ky_ref[pl.ds(first, value.shape[0]), :] = value

        kron_eye(tyf_ref[gy], CH, put)

    @pl.when(half == 0)
    def _():
        for cs in range(2):
            def put(first, value, cs=cs):
                kx_ref[step, cs, pl.ds(first, value.shape[0]), :] = value
            kron_eye(txf_ref[gx, step, cs], MZ, put)

    lhs = jnp.concatenate(
        [fields_ref[g].reshape(yl * CH, fields_ref.shape[-1]) for g in range(G)], axis=-1
    )
    amplitude = dot(lhs, depth_ref[...]).astype(BF)
    turned = dot(ky_ref[...], amplitude).astype(BF)
    top = MY * CH
    term = dot(turned[:top], kx_ref[step, 0]) + dot(turned[top:], kx_ref[step, 1])

    @pl.when(step == 0)
    def _():
        total_ref[...] = term

    @pl.when(step > 0)
    def _():
        total_ref[...] += term

    def scatter(h, i):
        px, py, _ = target(i * n_col)
        return pltpu.make_async_remote_copy(
            src_ref=send_ref.at[h, px, py], dst_ref=recv_ref.at[h, i],
            send_sem=send1.at[h, i], recv_sem=recv1.at[h, i],
            device_id={"gx": px, "gy": py}, device_id_type=MESH,
        )

    def share(i):
        return pltpu.make_async_remote_copy(
            src_ref=wa_ref.at[col], dst_ref=wa_ref.at[col],
            send_sem=send2.at[i], recv_sem=recv2.at[i],
            device_id={"col": target(i)[2]}, device_id_type=MESH,
        )

    @pl.when((half == 0) & (step == min(1, steps - 1)))
    def _():
        weights_copy.wait()
        eye = (iota((C, C), 0) == iota((C, C), 1)).astype(F32).astype(BF)
        for k in range(kyl):
            for d in range(dl):
                parts = [w_ref[j, k, r, d] for r in range(2) for j in range(kxl)]
                wa_ref[col, k, d] = lax.dot_general(
                    eye, jnp.concatenate(parts, axis=0), (((1,), (1,)), ((), ())),
                    preferred_element_type=F32,
                ).astype(BF)
        pl.semaphore_wait(pltpu.get_barrier_semaphore(), nxy + n_col - 2)
        for i in range(1, n_col):
            share(i).start()

    @pl.when(step == steps - 1)
    def _():
        rows = kyl * CH
        for b in range(n_gx):
            block = total_ref[:, b * L:(b + 1) * L].astype(BF)
            for q in range(n_gy):
                send_ref[half, b, q] = block[q * rows:(q + 1) * rows]

        loop(1, nxy, lambda i: scatter(half, i).start())

    @pl.when((half == halves - 1) & (step == steps - 1))
    def _():
        for cs in range(2):
            def put(first, value, cs=cs):
                gx_ref[cs, pl.ds(first, value.shape[0]), :] = value
            kron_eye(txi_ref[gx, cs], MZ, put)
        chunk = min(256, yl * CH)
        for first in range(0, yl * CH, chunk):
            hy_ref[pl.ds(first, chunk), :] = expand(
                tyi_ref[gy], chunk, 2 * MY * CH,
                lambda i: div(i, CH),
                lambda j: div(j, per * kyl * dl) * kyl + mod(div(j, dl), kyl),
                lambda i: mod(i, CH),
                lambda j: mod(div(j, kyl * dl), per) * dl + mod(j, dl),
                first,
            )
        shape = (MY * C, MY * C)
        i, j = iota(shape, 0), iota(shape, 1)
        in_half = mod(i, MY * CH)
        gy_i = div(in_half, per * kyl * dl)
        col_i = div(i, MY * CH) * per + mod(div(in_half, kyl * dl), per)
        source = (gy_i * n_col + col_i) * (kyl * dl) + mod(in_half, kyl * dl)
        same = (gy_i == div(j, n_col * kyl * dl)) & (mod(div(i, dl), kyl) == mod(div(j, dl), kyl))
        cm_ref[...] = (
            (source == j).astype(F32) - jnp.where(same, 1.0 / C, 0.0)
        ).astype(BF)

        sums = {}
        for h in range(halves):
            total = send_ref[h, gx, gy].astype(F32)
            for i in range(1, nxy):
                scatter(h, i).wait_recv()
                total = total + recv_ref[h, i].astype(F32)
            spec = total.astype(BF).astype(F32)
            if h == 0:
                for i in range(1, n_col):
                    share(i).wait_recv()
            re, im = spec[:, :L // 2], spec[:, L // 2:]
            re = jnp.concatenate([re, re], axis=-1)
            im = jnp.concatenate([im, im], axis=-1)
            for q in range(n_col):
                for k in range(kyl):
                    rows, chans = slice(k * CH, (k + 1) * CH), slice(h * CH, (h + 1) * CH)
                    weight = wa_ref[q, k, :, chans].astype(F32)
                    new = [jnp.sum(v[rows][None] * weight, axis=1) for v in (re, im)]
                    old = sums.get((q, k))
                    sums[q, k] = new if old is None else [a + b for a, b in zip(old, new)]
        for q in range(n_col):
            for k in range(kyl):
                first, second = sums[q, k]
                turned_second = jnp.concatenate(
                    [-second[:, L // 2:], second[:, :L // 2]], axis=-1
                )
                row = (q * kyl + k) * dl
                mix_ref[row:row + dl] = (first + turned_second).astype(BF)
        modes_ref[gx, gy] = mix_ref[...]

        def gather(i):
            px, py, _ = target(i * n_col)
            return pltpu.make_async_remote_copy(
                src_ref=mix_ref, dst_ref=modes_ref.at[gx, gy],
                send_sem=send3.at[i], recv_sem=recv3.at[i],
                device_id={"gx": px, "gy": py}, device_id_type=MESH,
            )

        loop(1, nxy, lambda i: gather(i).start())
        for h in range(halves):
            loop(1, nxy, lambda i: scatter(h, i).wait_send())
        for i in range(1, n_col):
            share(i).wait_send()
        loop(1, nxy, lambda i: gather(i).wait_recv())
        full = jnp.concatenate(
            [modes_ref[b].reshape(MY * C, L) for b in range(n_gx)], axis=-1
        )
        full = dot(cm_ref[...], full).astype(BF)
        for h in range(halves):
            part = full[h * MY * CH:(h + 1) * MY * CH]
            part = jnp.concatenate([dot(part, gx_ref[cs]).astype(BF) for cs in range(2)], axis=0)
            out_ref[:, h * CH:(h + 1) * CH] = dot(hy_ref[...], part).astype(BF).reshape(
                yl, CH, out_ref.shape[-1]
            )
        loop(1, nxy, lambda i: gather(i).wait_send())


def back_kernel(
    sizes, rows_ref, fields_ref, depth_ref, skip_ref, bias_ref, gain_ref, shift_ref, out_ref, wbd_ref
):
    G, C, MZ, Z, rows, tile = sizes

    @pl.when(pl.program_id(0) == 0)
    def _():
        weight = skip_ref[...].astype(F32)
        weight = (weight - jnp.mean(weight, axis=0, keepdims=True)).astype(BF)
        wbd_ref[...] = expand(
            weight, tile, tile,
            lambda i: mod(i, C), lambda j: mod(j, C), lambda i: div(i, C), lambda j: div(j, C),
        )

    def column(ref):
        return jnp.sum(jnp.where(iota((C, C), 0) == iota((C, C), 1), ref[...], 0.0), 1, keepdims=True)

    bias = column(bias_ref)
    bias = (bias - jnp.mean(bias, axis=0, keepdims=True))[None]
    gain = column(gain_ref)[None]
    shift = column(shift_ref)[None]
    for first in range(0, rows, tile):
        for x in range(0, G, 2):
            hidden = jnp.concatenate(
                [fields_ref[x + k, first:first + tile] for k in range(2)], axis=-1
            )
            pre = dot(wbd_ref[...], hidden) + dot(
                rows_ref[first:first + tile, x * 2 * MZ:(x + 2) * 2 * MZ], depth_ref[...]
            )
            pre = pre.reshape(tile // C, C, 2 * Z) + bias
            spread = jnp.mean(pre * pre, axis=1, keepdims=True)
            normed = pre * (lax.rsqrt(spread + norm_eps) * gain) + shift
            value = (0.5 * normed) * (1.0 + lax.erf(normed * (0.5 ** 0.5)))
            value = value.astype(BF).reshape(tile, 2 * Z)
            for k in range(2):
                out_ref[x + k, first:first + tile] = value[:, k * Z:(k + 1) * Z]


def build(mesh):
    n_gx, n_gy, n_col = (mesh.shape[a] for a in ("gx", "gy", "col"))

    def local(fields, spectral, skip_weight, skip_bias, norm_gain, norm_shift):
        hidden = fields[0]
        xl, yl, C, Z = hidden.shape
        weights = spectral[0]
        kxl, kyl, _, _, dl, MZ = weights.shape
        X, Y, MX, MY = xl * n_gx, yl * n_gy, kxl * n_gx, kyl * n_gy
        G = min(8, xl)
        steps = xl // G
        L = 2 * kxl * MZ
        N, nxy = n_gx * n_gy * n_col, n_gx * n_gy

        cz, sz = cos_sin(np.arange(Z), np.arange(MZ), Z)
        forward = np.concatenate([cz, -sz], axis=1)
        depth_forward = np.kron(np.eye(G), forward)
        backward = np.concatenate([cz.T, -sz.T], axis=0) / math.sqrt(MX * MY * MZ)
        depth_backward = np.kron(np.eye(2), backward)
        cy, sy = cos_sin(np.arange(Y), signed(MY), Y)
        tyf = np.stack([cy, sy]).reshape(2, n_gy, yl, MY).transpose(1, 0, 3, 2)
        tyf = tyf.reshape(n_gy, 2 * MY, yl)
        tyi = np.stack([cy, sy]).reshape(2, n_gy, yl, MY).transpose(1, 2, 0, 3)
        tyi = tyi.reshape(n_gy, yl, 2 * MY)
        cx, sx = cos_sin(np.arange(X), signed(MX), X)
        f = np.stack([
            np.stack([np.stack([cx, -sx], 1), np.stack([sx, cx], 1)], 1),
            np.stack([np.stack([-sx, -cx], 1), np.stack([cx, -sx], 1)], 1),
        ]) / math.sqrt(X * Y * Z)
        f = f.reshape(2, n_gx, steps, G, 2, 2, n_gx, kxl).transpose(1, 2, 0, 3, 4, 6, 5, 7)
        txf = f.reshape(n_gx, steps, 2, 2 * G, 2 * MX)
        b = np.stack([
            np.stack([np.stack([cx, sx]), np.stack([-sx, cx])]),
            np.stack([np.stack([-sx, cx]), np.stack([-cx, -sx])]),
        ])
        b = b.reshape(2, 2, 2, n_gx, xl, n_gx, kxl).transpose(3, 0, 5, 1, 6, 4, 2)
        txi = b.reshape(n_gx, 2, 2 * MX, 2 * xl)
        const = lambda a: jnp.asarray(a.astype(np.float32)).astype(BF)

        cells = hidden.reshape(xl, yl * C, Z)
        halves = 2 if C % 32 == 0 and n_col % 2 == 0 else 1
        CH = C // halves
        turned = jnp.transpose(weights, (0, 1, 2, 4, 5, 3))

        def whole(shape):
            return pl.BlockSpec(shape, lambda *_: (0,) * len(shape))

        sizes = (n_gx, n_gy, n_col, xl, yl, C, MY, MZ, kxl, kyl, dl, G, steps, halves)
        tables = [const(t) for t in (depth_forward, tyf, txf, txi, tyi)]
        rows_both = pl.pallas_call(
            functools.partial(front_kernel, sizes),
            grid=(halves, steps),
            out_shape=jax.ShapeDtypeStruct((yl, C, xl * 2 * MZ), BF),
            in_specs=[
                pl.BlockSpec((G, yl, CH, Z), lambda h, i: (i, 0, h, 0)),
                pl.BlockSpec(memory_space=pl.ANY),
            ] + [whole(t.shape) for t in tables],
            out_specs=whole((yl, C, xl * 2 * MZ)),
            scratch_shapes=[
                pltpu.VMEM((2 * MY * CH, yl * CH), BF),
                pltpu.VMEM((steps, 2, G * 2 * MZ, 2 * MX * MZ), BF),
                pltpu.VMEM((MY * CH, 2 * MX * MZ), F32),
                pltpu.VMEM((halves, n_gx, n_gy, kyl * CH, L), BF),
                pltpu.VMEM((halves, nxy, kyl * CH, L), BF),
                pltpu.VMEM((kyl * C, L), BF),
                pltpu.VMEM((n_gx, n_gy, kyl * C, L), BF),
                pltpu.VMEM((2, 2 * MX * MZ, 2 * xl * MZ), BF),
                pltpu.VMEM((yl * CH, 2 * MY * CH), BF),
                pltpu.VMEM((MY * C, MY * C), BF),
                pltpu.VMEM(turned.shape, BF),
                pltpu.VMEM((n_col, kyl, dl, C, L), BF),
                pltpu.SemaphoreType.DMA,
                pltpu.SemaphoreType.DMA((halves, nxy)),
                pltpu.SemaphoreType.DMA((halves, nxy)),
                pltpu.SemaphoreType.DMA((n_col,)),
                pltpu.SemaphoreType.DMA((n_col,)),
                pltpu.SemaphoreType.DMA((nxy,)),
                pltpu.SemaphoreType.DMA((nxy,)),
            ],
            compiler_params=pltpu.CompilerParams(
                collective_id=0, has_side_effects=True, vmem_limit_bytes=60 * 2**20,
                dimension_semantics=("arbitrary", "arbitrary"),
            ),
            name="front",
        )(hidden, turned, *tables).reshape(yl * C, xl * 2 * MZ)

        G2 = min(4, xl)
        rows = yl * C
        tile = min(256, rows)
        out = pl.pallas_call(
            functools.partial(back_kernel, (G2, C, MZ, Z, rows, tile)),
            grid=(xl // G2,),
            out_shape=jax.ShapeDtypeStruct(cells.shape, BF),
            in_specs=[
                pl.BlockSpec((rows, G2 * 2 * MZ), lambda i: (0, i)),
                pl.BlockSpec((G2, rows, Z), lambda i: (i, 0, 0)),
                whole((4 * MZ, 2 * Z)), whole((C, C)), whole((1, C)), whole((1, C)), whole((1, C)),
            ],
            out_specs=pl.BlockSpec((G2, rows, Z), lambda i: (i, 0, 0)),
            scratch_shapes=[pltpu.VMEM((tile, tile), BF)],
            compiler_params=pltpu.CompilerParams(
                vmem_limit_bytes=60 * 2**20, dimension_semantics=("arbitrary",)
            ),
            name="back",
        )(
            rows_both, cells, const(depth_backward), skip_weight[0],
            skip_bias, norm_gain, norm_shift,
        )
        return out.reshape(1, xl, yl, C, Z)

    return local


def solution(mesh):
    placed = (
        P("col", "gx", "gy", None, None),
        P(None, "gx", "gy", None, None, "col", None),
        P(), P(), P(), P(),
    )
    return jax.shard_map(
        build(mesh), mesh=mesh, in_specs=placed,
        out_specs=P("col", "gx", "gy", None, None), check_vma=False,
    )
```

profile of v0, /device:TPU:1, one launch (start us, length us, event | category | flops | bytes accessed | tf_op | source)
XLA Modules:
  0.0 57.2 jit_solution(13501803903032415468)
XLA Ops:
  0.0 43.3 %front.1 = bf16[32,32,1024]{2,1,0:T(8,128)(2,1)} custom-call(bf16[32,32,32,128]{3,2,1,0:T(8,128)(2,1)} %bitcast.8, bf16[4,4,2,16,16,32]{5,4,3,2,1,0:T(8,128)(2,1)} %bitcast.11, bf16[1024,256]{1,0:T(8,128)(2,1)} %constant.19.depth_ref, bf16[4,32,32]{2,1,0:T(8,128)(2,1)} %constant.20.tyf_ref, bf16[4,4,2,16,32]{4,3,2,1,0:T(8,128)(2,1)} %constant.21.txf_ref, ...), custom_call_target="tpu_custom_call" | custom-call | tf_op jit(solution)/shard_map/front/pallas_call | solution.py:366
  43.3 13.8 %back.1 = bf16[32,1024,128]{2,1,0:T(8,128)(2,1)} custom-call(bf16[1024,1024]{1,0:T(8,128)(2,1)} %bitcast.10, bf16[32,1024,128]{2,1,0:T(8,128)(2,1)} %bitcast.9, bf16[64,256]{1,0:T(8,128)(2,1)} %constant.24.depth_ref, bf16[32,32]{1,0:T(8,128)(2,1)} %bitcast.12, f32[1,32]{1,0:T(1,128)} %bias_ref.1, f32[1,32]{1,0:T(1,128)} %gain_ref.1, f32[1,32]{1,0:T(1,128)} %shift_ref.1), custom_call_target="tpu_custom_call" | custom-call | tf_op jit(solution)/shard_map/back/pallas_call | solution.py:406
where the time goes:
time: 58 us; the launch traced here: 57.2 us
  Pallas kernels  57.1 us (98%)
    pallas_call x1, Pallas kernels, local(): pl.pallas_call(functools.partial(front_kernel, sizes), grid=(halves, step...  43.3 us
    pallas_call x1, Pallas kernels, local(): pl.pallas_call(functools.partial(back_kernel, (G2, C, MZ, Z, rows, tile))...  13.8 us

commit v1 on v0

v1 whole, which is shorter than its diff:
```python
import functools
import math

import jax
import jax.numpy as jnp
import numpy as np
from jax import lax
from jax.experimental import pallas as pl
from jax.experimental.pallas import tpu as pltpu
from jax.sharding import PartitionSpec as P

norm_eps = 1e-05
BF = jnp.bfloat16
F32 = jnp.float32
MESH = pl.DeviceIdType.MESH


def signed(count):
    index = np.arange(count)
    return np.where(index < count // 2, index, index - count)


def cos_sin(positions, frequency, length):
    turns = (positions[:, None] * frequency[None, :]) % length
    phase = turns * (2.0 * math.pi / length)
    return np.cos(phase), np.sin(phase)


def log2(n):
    assert n & (n - 1) == 0
    return n.bit_length() - 1


def div(i, n):
    return lax.shift_right_logical(i, jnp.int32(log2(n)))


def mod(i, n):
    return lax.bitwise_and(i, jnp.int32(n - 1))


def iota(shape, dim):
    return lax.broadcasted_iota(jnp.int32, shape, dim)


def dot(a, b):
    return jnp.dot(a, b, preferred_element_type=F32)


def spread_table(table, width, pick):
    r, c = table.shape
    right = (iota((c, width), 0) == pick(iota((c, width), 1))).astype(F32).astype(BF)
    return dot(table, right)


def band(store, table_ref, rows, height, keep):
    for m in range(rows):
        store(m * height, jnp.where(keep, table_ref[m:m + 1, :], 0.0).astype(BF))


def front_kernel(
    sizes,
    fields_hbm, spectral_hbm, depth_ref, tyf_ref, txf_ref, txi_ref, tyi_ref, skip_ref, bias_ref,
    rows_ref, pre_ref,
    fields_ref, ky_ref, kx_ref, amp_ref, turn_ref, total_ref,
    swap_ref, take_ref, send_ref, recv_ref, mix_ref, modes_ref, gx_ref, hy_ref, w_ref, wa_ref,
    wbd_ref, ty_ref, tx_ref, ti_ref, th_ref,
    fsem, wsem, swap_s, swap_r, send1, recv1, send2, recv2, send3, recv3, send4, recv4,
):
    n_gx, n_gy, n_col, xl, yl, C, MY, MZ, kxl, kyl, dl, G, steps, halves, tile = sizes
    n_hi = n_gy // 2
    peers = n_gx * n_hi
    MX = n_gx * kxl
    L = 2 * kxl * MZ
    CH = C // halves
    per = n_col // halves
    Z = fields_ref.shape[-1]
    block = kyl * CH
    top = MY * CH
    gx, gy, col = lax.axis_index("gx"), lax.axis_index("gy"), lax.axis_index("col")
    lo, hi = lax.rem(gy, 2), lax.div(gy, 2)
    mate = gy + 1 - 2 * lo
    unrolled = peers <= 16

    def peer(i):
        return lax.rem(gx + i // n_hi, n_gx), lax.rem(hi + i % n_hi, n_hi)

    def source(i):
        return lax.rem(gx + n_gx - i // n_hi, n_gx), lax.rem(hi + n_hi - i % n_hi, n_hi)

    def side(i):
        return lax.rem(col + i, n_col)

    def loop(low, high, body):
        if unrolled:
            for i in range(low, high):
                body(i)
            return

        def go(i, carry):
            body(i)
            return carry
        lax.fori_loop(low, high, go, 0)

    def field_copy(h, s):
        at = (pl.ds(s * G, G), slice(None), pl.ds(h * CH, CH), slice(None))
        return pltpu.make_async_copy(fields_hbm.at[at], fields_ref.at[at], fsem.at[h, s])

    weights_copy = pltpu.make_async_copy(spectral_hbm, w_ref, wsem)
    units = [(h, s) for h in range(halves) for s in range(steps)]
    field_copy(*units[0]).start()
    weights_copy.start()
    for unit in units[1:]:
        field_copy(*unit).start()

    barrier = pltpu.get_barrier_semaphore()

    def greet(i):
        px, ph = peer(i)
        pl.semaphore_signal(
            barrier, inc=1, device_id={"gx": px, "gy": 2 * ph + lo}, device_id_type=MESH
        )

    def greet_side(i):
        pl.semaphore_signal(barrier, inc=1, device_id={"col": side(i)}, device_id_type=MESH)

    loop(1, peers, greet)
    loop(1, n_col, greet_side)
    pl.semaphore_signal(barrier, inc=1, device_id={"gy": mate}, device_id_type=MESH)

    ty_ref[...] = spread_table(tyf_ref[gy], yl * CH, lambda j: div(j, CH))
    tx_ref[...] = spread_table(txf_ref[gx], 2 * MX * MZ, lambda j: div(j, MZ))

    def put_ky(first, value):
        ky_ref[pl.ds(first, CH), :] = value

    band(put_ky, ty_ref, 2 * MY, CH, iota((CH, yl * CH), 0) == mod(iota((CH, yl * CH), 1), CH))

    def put_kx(first, value):
        kx_ref[pl.ds(first, MZ), :] = value

    wide = 2 * MX * MZ
    band(put_kx, tx_ref, 4 * steps * G, MZ, iota((MZ, wide), 0) == mod(iota((MZ, wide), 1), MZ))

    def share(i):
        return pltpu.make_async_remote_copy(
            src_ref=wa_ref.at[col], dst_ref=wa_ref.at[col],
            send_sem=send2.at[i], recv_sem=recv2.at[i],
            device_id={"col": side(i)}, device_id_type=MESH,
        )

    def swap(h):
        return pltpu.make_async_remote_copy(
            src_ref=swap_ref.at[h], dst_ref=take_ref.at[h],
            send_sem=swap_s.at[h], recv_sem=swap_r.at[h],
            device_id={"gy": mate}, device_id_type=MESH,
        )

    def scatter(h, i):
        px, ph = peer(i)
        return pltpu.make_async_remote_copy(
            src_ref=send_ref.at[h, px, ph], dst_ref=recv_ref.at[h, i],
            send_sem=send1.at[h, i], recv_sem=recv1.at[h, i],
            device_id={"gx": px, "gy": 2 * ph + lo}, device_id_type=MESH,
        )

    def gather(i):
        px, ph = peer(i)
        return pltpu.make_async_remote_copy(
            src_ref=mix_ref, dst_ref=modes_ref.at[gx, gy],
            send_sem=send3.at[i], recv_sem=recv3.at[i],
            device_id={"gx": px, "gy": 2 * ph + lo}, device_id_type=MESH,
        )

    def relay(i):
        if isinstance(i, int) and i == 0:
            src, at = mix_ref, modes_ref.at[gx, gy]
        else:
            sx, sh = source(i)
            src = at = modes_ref.at[sx, 2 * sh + lo]
        return pltpu.make_async_remote_copy(
            src_ref=src, dst_ref=at, send_sem=send4.at[i], recv_sem=recv4.at[i],
            device_id={"gy": mate}, device_id_type=MESH,
        )

    def prepare_weights():
        weights_copy.wait()
        eye = (iota((C, C), 0) == iota((C, C), 1)).astype(F32).astype(BF)
        for k in range(kyl):
            for d in range(dl):
                parts = [w_ref[j, k, r, d] for r in range(2) for j in range(kxl)]
                wa_ref[col, k, d] = lax.dot_general(
                    eye, jnp.concatenate(parts, axis=0), (((1,), (1,)), ((), ())),
                    preferred_element_type=F32,
                ).astype(BF)
        pl.semaphore_wait(barrier, peers + n_col - 1)
        for i in range(1, n_col):
            share(i).start()

    def z_stage(u):
        h, s = units[u]
        field_copy(h, s).wait()
        lhs = jnp.concatenate(
            [fields_ref[s * G + g, :, h * CH:(h + 1) * CH, :].reshape(yl * CH, Z) for g in range(G)],
            axis=-1,
        )
        amp_ref[u % 2] = dot(lhs, depth_ref[...]).astype(BF)

    def y_stage(u):
        h, s = units[u]
        lanes = 2 * G * MZ
        turn_ref[h % 2, :, s * lanes:(s + 1) * lanes] = dot(ky_ref[...], amp_ref[u % 2]).astype(BF)

    piece = min(2, steps)

    def x_stage(u):
        h, s = units[u]
        if s % piece != piece - 1:
            return
        lanes = piece * 2 * G * MZ
        cut = slice((s + 1) * 2 * G * MZ - lanes, (s + 1) * 2 * G * MZ)
        count = steps * 2 * G * MZ
        term = dot(turn_ref[h % 2, :top, cut], kx_ref[cut.start:cut.stop, :])
        term = term + dot(turn_ref[h % 2, top:, cut], kx_ref[count + cut.start:count + cut.stop, :])
        if s == piece - 1:
            total_ref[h % 2] = term
        else:
            total_ref[h % 2] += term
        if s == steps - 1:
            for i in range(n_hi):
                at = pl.multiple_of((2 * i + 1 - lo) * block, block)
                swap_ref[h, i] = total_ref[h % 2, pl.ds(at, block), :].astype(BF)
            swap(h).start()

    def send_half(h):
        swap(h).wait_recv()
        for i in range(n_hi):
            at = pl.multiple_of((2 * i + lo) * block, block)
            value = total_ref[h % 2, pl.ds(at, block), :] + take_ref[h, i].astype(F32)
            value = value.astype(BF)
            for b in range(n_gx):
                send_ref[h, b, i] = value[:, b * L:(b + 1) * L]
        loop(1, peers, lambda i: scatter(h, i).start())

    ready = min(2, len(units))
    for u in range(len(units) + 2):
        if u == ready:
            prepare_weights()
        if u < len(units):
            z_stage(u)
        if 0 <= u - 1 < len(units):
            y_stage(u - 1)
        if 0 <= u - 2:
            x_stage(u - 2)
        if halves > 1 and u == steps + 3:
            send_half(0)

    weight = skip_ref[...].astype(F32)
    weight = (weight - jnp.mean(weight, axis=0, keepdims=True)).astype(BF)
    tall = spread_table(weight, tile, lambda j: mod(j, C))
    for g in range(tile // C):
        keep = div(iota((C, tile), 1), C) == g
        wbd_ref[g * C:(g + 1) * C, :] = jnp.where(keep, tall, 0.0).astype(BF)
    diagonal = iota((C, C), 0) == iota((C, C), 1)
    bias = jnp.sum(jnp.where(diagonal, bias_ref[...], 0.0), 1, keepdims=True)
    bias = (bias - jnp.mean(bias, axis=0, keepdims=True))[None]

    def skip_cells(low, high):
        def go(i, carry):
            x = 2 * i
            for y in range(0, yl, tile // C):
                hidden = jnp.concatenate(
                    [fields_ref[x + k, y:y + tile // C].reshape(tile, Z) for k in range(2)], axis=-1
                )
                part = dot(wbd_ref[...], hidden).reshape(tile // C, C, 2 * Z) + bias
                for k in range(2):
                    pre_ref[x + k, y:y + tile // C] = part[:, :, k * Z:(k + 1) * Z]
            return carry
        lax.fori_loop(low, high, go, 0)

    pairs = xl // 2
    skip_cells(0, pairs // 8)
    send_half(halves - 1)

    ti_ref[...] = spread_table(txi_ref[gx], 2 * xl * MZ, lambda j: div(j, MZ))
    th_ref[...] = spread_table(
        tyi_ref[gy], 2 * MY * CH,
        lambda j: div(j, per * kyl * dl) * kyl + mod(div(j, dl), kyl),
    )

    def put_gx(first, value):
        gx_ref[pl.ds(first, MZ), :] = value

    wide = 2 * xl * MZ
    band(put_gx, ti_ref, 4 * MX, MZ, iota((MZ, wide), 0) == mod(iota((MZ, wide), 1), MZ))

    def put_hy(first, value):
        hy_ref[pl.ds(first, CH), :] = value

    j = iota((CH, 2 * MY * CH), 1)
    band(
        put_hy, th_ref, yl, CH,
        iota((CH, 2 * MY * CH), 0) == mod(div(j, kyl * dl), per) * dl + mod(j, dl),
    )
    skip_cells(pairs // 8, pairs // 2)

    sums = {}
    for h in range(halves):
        total = send_ref[h, gx, hi].astype(F32)
        for i in range(1, peers):
            scatter(h, i).wait_recv()
            total = total + recv_ref[h, i].astype(F32)
        spec = total.astype(BF).astype(F32)
        if h == 0:
            for i in range(1, n_col):
                share(i).wait_recv()
        re, im = spec[:, :L // 2], spec[:, L // 2:]
        re = jnp.concatenate([re, re], axis=-1)
        im = jnp.concatenate([im, im], axis=-1)
        for q in range(n_col):
            for k in range(kyl):
                rows, chans = slice(k * CH, (k + 1) * CH), slice(h * CH, (h + 1) * CH)
                weight = wa_ref[q, k, :, chans].astype(F32)
                new = [jnp.sum(v[rows][None] * weight, axis=1) for v in (re, im)]
                old = sums.get((q, k))
                sums[q, k] = new if old is None else [a + b for a, b in zip(old, new)]
    for k in range(kyl):
        mixed = []
        for q in range(n_col):
            first, second = sums[q, k]
            turned_second = jnp.concatenate(
                [-second[:, L // 2:], second[:, :L // 2]], axis=-1
            )
            mixed.append(first + turned_second)
        centre = sum(jnp.sum(m, axis=0, keepdims=True) for m in mixed) * (1.0 / C)
        for q in range(n_col):
            row = (q * kyl + k) * dl
            mix_ref[row:row + dl] = (mixed[q] - centre).astype(BF)

    loop(1, peers, lambda i: gather(i).start())
    relay(0).start()
    modes_ref[gx, gy] = mix_ref[...]
    skip_cells(pairs // 2, pairs)

    def pass_on(i):
        gather(i).wait_recv()
        relay(i).start()

    loop(1, peers, pass_on)
    for h in range(halves):
        swap(h).wait_send()
        loop(1, peers, lambda i: scatter(h, i).wait_send())
    for i in range(1, n_col):
        share(i).wait_send()
    relay(0).wait_recv()
    loop(1, peers, lambda i: relay(i).wait_recv())

    span = kyl * CH
    lanes = rows_ref.shape[-1]
    for h in range(halves):
        part = jnp.concatenate(
            [
                jnp.concatenate([modes_ref[b, g, h * span:(h + 1) * span] for g in range(n_gy)], axis=0)
                for b in range(n_gx)
            ],
            axis=-1,
        )
        half = 2 * MX * MZ
        part = jnp.concatenate(
            [dot(part, gx_ref[cs * half:(cs + 1) * half, :]).astype(BF) for cs in range(2)], axis=0
        )
        value = dot(hy_ref[...], part).astype(BF).reshape(yl, CH, 2 * xl * MZ)
        for g in range(rows_ref.shape[0]):
            rows_ref[g, :, h * CH:(h + 1) * CH] = value[:, :, g * lanes:(g + 1) * lanes]
    relay(0).wait_send()
    loop(1, peers, lambda i: gather(i).wait_send())
    loop(1, peers, lambda i: relay(i).wait_send())


def back_kernel(sizes, rows_ref, pre_ref, depth_ref, gain_ref, shift_ref, out_hbm, out_ref, sem):
    groups, G, yl, C, Z, cells = sizes

    def column(ref):
        return jnp.sum(jnp.where(iota((C, C), 0) == iota((C, C), 1), ref[...], 0.0), 1, keepdims=True)

    root = 0.5 ** 0.5
    gain = (column(gain_ref) * root)[None]
    shift = (column(shift_ref) * root)[None]

    def leave(i, slot):
        return pltpu.make_async_copy(
            out_ref.at[slot], out_hbm.at[pl.ds(i * G, G)], sem.at[slot]
        )

    def go(i, carry):
        slot = mod(i, 2)

        @pl.when(i >= 2)
        def _():
            leave(i - 2, slot).wait()

        for y in range(0, yl, cells):
            part = dot(rows_ref[i, y:y + cells].reshape(cells * C, rows_ref.shape[-1]), depth_ref[...])
            for k in range(G):
                pre = part[:, k * Z:(k + 1) * Z].reshape(cells, C, Z) + pre_ref[i * G + k, y:y + cells]
                spread = jnp.mean(pre * pre, axis=1, keepdims=True)
                value = (pre * (lax.rsqrt(spread + norm_eps) * gain) + shift).astype(BF)
                value = (value * root).astype(BF) * (1.0 + lax.erf(value)).astype(BF)
                out_ref[slot, k, y:y + cells] = value
        leave(i, slot).start()
        return carry

    lax.fori_loop(0, groups, go, 0)
    for i in range(max(0, groups - 2), groups):
        leave(i, i % 2).wait()


def build(mesh):
    n_gx, n_gy, n_col = (mesh.shape[a] for a in ("gx", "gy", "col"))

    def local(fields, spectral, skip_weight, skip_bias, norm_gain, norm_shift):
        hidden = fields[0]
        xl, yl, C, Z = hidden.shape
        weights = spectral[0]
        kxl, kyl, _, _, dl, MZ = weights.shape
        X, Y, MX, MY = xl * n_gx, yl * n_gy, kxl * n_gx, kyl * n_gy
        G = min(8, xl)
        steps = xl // G
        L = 2 * kxl * MZ
        n_hi = n_gy // 2
        peers = n_gx * n_hi
        G2 = min(4, xl)

        cz, sz = cos_sin(np.arange(Z), np.arange(MZ), Z)
        forward = np.concatenate([cz, -sz], axis=1)
        depth_forward = np.kron(np.eye(G), forward)
        backward = np.concatenate([cz.T, -sz.T], axis=0) / math.sqrt(MX * MY * MZ)
        depth_backward = np.kron(np.eye(G2), backward)
        cy, sy = cos_sin(np.arange(Y), signed(MY), Y)
        tyf = np.stack([cy, sy]).reshape(2, n_gy, yl, MY).transpose(1, 0, 3, 2)
        tyf = tyf.reshape(n_gy, 2 * MY, yl)
        tyi = np.stack([cy, sy]).reshape(2, n_gy, yl, MY).transpose(1, 2, 0, 3)
        tyi = tyi.reshape(n_gy, yl, 2 * MY)
        cx, sx = cos_sin(np.arange(X), signed(MX), X)
        f = np.stack([
            np.stack([np.stack([cx, -sx], 1), np.stack([sx, cx], 1)], 1),
            np.stack([np.stack([-sx, -cx], 1), np.stack([cx, -sx], 1)], 1),
        ]) / math.sqrt(X * Y * Z)
        f = f.reshape(2, n_gx, xl, 2, 2, n_gx, kxl).transpose(1, 0, 2, 3, 5, 4, 6)
        txf = f.reshape(n_gx, 4 * xl, 2 * MX)
        b = np.stack([
            np.stack([np.stack([cx, sx]), np.stack([-sx, cx])]),
            np.stack([np.stack([-sx, cx]), np.stack([-cx, -sx])]),
        ])
        b = b.reshape(2, 2, 2, n_gx, xl, n_gx, kxl).transpose(3, 0, 5, 1, 6, 4, 2)
        txi = b.reshape(n_gx, 4 * MX, 2 * xl)
        const = lambda a: jnp.asarray(a.astype(np.float32)).astype(BF)

        halves = 2 if C % 32 == 0 and n_col % 2 == 0 else 1
        CH = C // halves
        turned = jnp.transpose(weights, (0, 1, 2, 4, 5, 3))
        tile = min(256, yl * C)

        sizes = (n_gx, n_gy, n_col, xl, yl, C, MY, MZ, kxl, kyl, dl, G, steps, halves, tile)
        tables = [const(t) for t in (depth_forward, tyf, txf, txi, tyi)]
        inside = pl.BlockSpec(memory_space=pltpu.VMEM)
        outside = pl.BlockSpec(memory_space=pltpu.HBM)
        rows_both, pre = pl.pallas_call(
            functools.partial(front_kernel, sizes),
            out_shape=(
                pltpu.VMEM((xl // G2, yl, C, G2 * 2 * MZ), BF),
                pltpu.VMEM((xl, yl, C, Z), F32),
            ),
            in_specs=[outside, outside] + [inside] * (len(tables) + 2),
            out_specs=(inside, inside),
            scratch_shapes=[
                pltpu.VMEM((xl, yl, C, Z), BF),
                pltpu.VMEM((2 * MY * CH, yl * CH), BF),
                pltpu.VMEM((4 * xl * MZ, 2 * MX * MZ), BF),
                pltpu.VMEM((2, yl * CH, G * 2 * MZ), BF),
                pltpu.VMEM((2, 2 * MY * CH, xl * 2 * MZ), BF),
                pltpu.VMEM((2, MY * CH, 2 * MX * MZ), F32),
                pltpu.VMEM((halves, n_hi, kyl * CH, n_gx * L), BF),
                pltpu.VMEM((halves, n_hi, kyl * CH, n_gx * L), BF),
                pltpu.VMEM((halves, n_gx, n_hi, kyl * CH, L), BF),
                pltpu.VMEM((halves, peers, kyl * CH, L), BF),
                pltpu.VMEM((kyl * C, L), BF),
                pltpu.VMEM((n_gx, n_gy, kyl * C, L), BF),
                pltpu.VMEM((4 * MX * MZ, 2 * xl * MZ), BF),
                pltpu.VMEM((yl * CH, 2 * MY * CH), BF),
                pltpu.VMEM(turned.shape, BF),
                pltpu.VMEM((n_col, kyl, dl, C, L), BF),
                pltpu.VMEM((tile, tile), BF),
                pltpu.VMEM((2 * MY, yl * CH), F32),
                pltpu.VMEM((4 * xl, 2 * MX * MZ), F32),
                pltpu.VMEM((4 * MX, 2 * xl * MZ), F32),
                pltpu.VMEM((yl, 2 * MY * CH), F32),
                pltpu.SemaphoreType.DMA((halves, steps)),
                pltpu.SemaphoreType.DMA,
                pltpu.SemaphoreType.DMA((halves,)),
                pltpu.SemaphoreType.DMA((halves,)),
                pltpu.SemaphoreType.DMA((halves, peers)),
                pltpu.SemaphoreType.DMA((halves, peers)),
                pltpu.SemaphoreType.DMA((n_col,)),
                pltpu.SemaphoreType.DMA((n_col,)),
                pltpu.SemaphoreType.DMA((peers,)),
                pltpu.SemaphoreType.DMA((peers,)),
                pltpu.SemaphoreType.DMA((peers,)),
                pltpu.SemaphoreType.DMA((peers,)),
            ],
            compiler_params=pltpu.CompilerParams(
                collective_id=0, has_side_effects=True, vmem_limit_bytes=40 * 2**20,
            ),
            name="front",
        )(hidden, turned, *tables, skip_weight[0], skip_bias)

        groups = xl // G2
        cells = min(8, yl)
        out = pl.pallas_call(
            functools.partial(back_kernel, (groups, G2, yl, C, Z, cells)),
            out_shape=jax.ShapeDtypeStruct(hidden.shape, BF),
            in_specs=[inside] * 5,
            out_specs=outside,
            scratch_shapes=[
                pltpu.VMEM((2, G2, yl, C, Z), BF),
                pltpu.SemaphoreType.DMA((2,)),
            ],
            compiler_params=pltpu.CompilerParams(vmem_limit_bytes=12 * 2**20),
            name="back",
        )(rows_both, pre, const(depth_backward), norm_gain, norm_shift)
        return out[None]

    return local


def solution(mesh):
    placed = (
        P("col", "gx", "gy", None, None),
        P(None, "gx", "gy", None, None, "col", None),
        P(), P(), P(), P(),
    )
    return jax.shard_map(
        build(mesh), mesh=mesh, in_specs=placed,
        out_specs=P("col", "gx", "gy", None, None), check_vma=False,
    )
```

time: 58 us -> 45.6 us (0.79); the launches traced: 57.2 us -> 45.5 us
  Pallas kernels: 57.1 us -> 45.5 us
    pallas_call x2, Pallas kernels: 57.1 us -> 45.5 us  [the longest x1 34.7 us: local(): pl.pallas_call(functools.partial(front_kernel, sizes), out_shape=(pltpu.V...]
where the time goes in v1:
time: 45.6 us; the launch traced here: 45.5 us
  Pallas kernels  45.5 us (100%)
    pallas_call x1, Pallas kernels, local(): pl.pallas_call(functools.partial(front_kernel, sizes), out_shape=(pltpu.V...  34.7 us
    pallas_call x1, Pallas kernels, local(): pl.pallas_call(functools.partial(back_kernel, (groups, G2, yl, C, Z, cell...  10.8 us

profile of v1, /device:TPU:1, one launch (start us, length us, event | category | flops | bytes accessed | tf_op | source)
XLA Modules:
  0.0 45.5 jit_solution(8812917534110864514)
XLA Ops:
  0.0 0.0 copy-start
  0.0 0.0 copy-start.2
  0.0 0.0 copy-start.1
  0.0 34.7 %front.1 = (bf16[8,32,32,128]{3,2,1,0:T(8,128)(2,1)S(1)}, f32[32,32,32,128]{3,2,1,0:T(8,128)S(1)}) custom-call(bf16[32,32,32,128]{3,2,1,0:T(8,128)(2,1)} %bitcast.6, bf16[4,4,2,16,16,32]{5,4,3,2,1,0:T(8,128)(2,1)} %bitcast.7, bf16[1024,256]{1,0:T(8,128)(2,1)} %constant.19.depth_ref, bf16[4,32,32]{2,1,0:T(8,128)(2,1)} %constant.20.tyf_ref, ...), custom_call_target="tpu_custom_call" | custom-call | tf_op jit(solution)/shard_map/front/pallas_call | solution.py:468
  34.7 0.0 copy-done
  34.7 0.0 copy-done.2
  34.7 0.0 copy-done.1
  34.7 10.8 %back.1 = bf16[32,32,32,128]{3,2,1,0:T(8,128)(2,1)} custom-call(bf16[8,32,32,128]{3,2,1,0:T(8,128)(2,1)S(1)} %get-tuple-element.7.rows_ref, f32[32,32,32,128]{3,2,1,0:T(8,128)S(1)} %get-tuple-element.8.pre_ref, bf16[128,512]{1,0:T(8,128)(2,1)S(1)} %copy-done, f32[1,32]{1,0:T(1,128)S(1)} %copy-done.1, f32[1,32]{1,0:T(1,128)S(1)} %copy-done.2), custom_call_target="tpu_custom_call" | custom-call | tf_op jit(solution)/shard_map/back/pallas_call | solution.py:519
Async XLA Ops:
  0.0 34.7 %copy-start = (bf16[128,512]{1,0:T(8,128)(2,1)S(1)}, bf16[128,512]{1,0:T(8,128)(2,1)}, u32[]{:S(2)}) copy-start(bf16[128,512]{1,0:T(8,128)(2,1)} %constant.24.depth_ref) | copy-start | bytes 393220
  0.0 34.7 %copy-start.2 = (f32[1,32]{1,0:T(1,128)S(1)}, f32[1,32]{1,0:T(1,128)}, u32[]{:S(2)}) copy-start(f32[1,32]{1,0:T(1,128)} %shift_ref.1) | copy-start | bytes 388
  0.0 34.7 %copy-start.1 = (f32[1,32]{1,0:T(1,128)S(1)}, f32[1,32]{1,0:T(1,128)}, u32[]{:S(2)}) copy-start(f32[1,32]{1,0:T(1,128)} %gain_ref.1) | copy-start | bytes 388

commit v2 on v1

--- a/solution.py
+++ b/solution.py
@@ -53,6 +53,10 @@
     return dot(table, right)
 
 
+def per_dl(dl, n_col, halves):
+    return n_col == halves and dl % 8 == 0
+
+
 def band(store, table_ref, rows, height, keep):
     for m in range(rows):
         store(m * height, jnp.where(keep, table_ref[m:m + 1, :], 0.0).astype(BF))
@@ -60,7 +64,7 @@
 
 def front_kernel(
     sizes,
-    fields_hbm, spectral_hbm, depth_ref, tyf_ref, txf_ref, txi_ref, tyi_ref, skip_ref, bias_ref,
+    fields_hbm, spectral_hbm, depth_ref, tyf_ref, txf_ref, txi_ref, tyi_ref, skip_ref, bias_ref, gain_ref,
     rows_ref, pre_ref,
     fields_ref, ky_ref, kx_ref, amp_ref, turn_ref, total_ref,
     swap_ref, take_ref, send_ref, recv_ref, mix_ref, modes_ref, gx_ref, hy_ref, w_ref, wa_ref,
@@ -73,6 +77,7 @@
     MX = n_gx * kxl
     L = 2 * kxl * MZ
     CH = C // halves
+    CS = 8 if CH % 8 == 0 else CH
     per = n_col // halves
     Z = fields_ref.shape[-1]
     block = kyl * CH
@@ -110,7 +115,7 @@
     units = [(h, s) for h in range(halves) for s in range(steps)]
     field_copy(*units[0]).start()
     weights_copy.start()
-    for unit in units[1:]:
+    for unit in units[1:3]:
         field_copy(*unit).start()
 
     barrier = pltpu.get_barrier_semaphore()
@@ -128,13 +133,13 @@
     loop(1, n_col, greet_side)
     pl.semaphore_signal(barrier, inc=1, device_id={"gy": mate}, device_id_type=MESH)
 
-    ty_ref[...] = spread_table(tyf_ref[gy], yl * CH, lambda j: div(j, CH))
+    ty_ref[...] = spread_table(tyf_ref[gy], yl * CS, lambda j: div(j, CS))
     tx_ref[...] = spread_table(txf_ref[gx], 2 * MX * MZ, lambda j: div(j, MZ))
 
     def put_ky(first, value):
-        ky_ref[pl.ds(first, CH), :] = value
-
-    band(put_ky, ty_ref, 2 * MY, CH, iota((CH, yl * CH), 0) == mod(iota((CH, yl * CH), 1), CH))
+        ky_ref[pl.ds(first, CS), :] = value
+
+    band(put_ky, ty_ref, 2 * MY, CS, iota((CS, yl * CS), 0) == mod(iota((CS, yl * CS), 1), CS))
 
     def put_kx(first, value):
         kx_ref[pl.ds(first, MZ), :] = value
@@ -142,10 +147,10 @@
     wide = 2 * MX * MZ
     band(put_kx, tx_ref, 4 * steps * G, MZ, iota((MZ, wide), 0) == mod(iota((MZ, wide), 1), MZ))
 
-    def share(i):
+    def share(i, k):
         return pltpu.make_async_remote_copy(
-            src_ref=wa_ref.at[col], dst_ref=wa_ref.at[col],
-            send_sem=send2.at[i], recv_sem=recv2.at[i],
+            src_ref=wa_ref.at[col, k], dst_ref=wa_ref.at[col, k],
+            send_sem=send2.at[i, k], recv_sem=recv2.at[i, k],
             device_id={"col": side(i)}, device_id_type=MESH,
         )
 
@@ -164,22 +169,26 @@
             device_id={"gx": px, "gy": 2 * ph + lo}, device_id_type=MESH,
         )
 
-    def gather(i):
+    span = kyl * C // halves
+
+    def gather(h, i):
         px, ph = peer(i)
+        cut = pl.ds(h * span, span)
         return pltpu.make_async_remote_copy(
-            src_ref=mix_ref, dst_ref=modes_ref.at[gx, gy],
-            send_sem=send3.at[i], recv_sem=recv3.at[i],
+            src_ref=mix_ref.at[cut], dst_ref=modes_ref.at[gx, gy, cut],
+            send_sem=send3.at[h, i], recv_sem=recv3.at[h, i],
             device_id={"gx": px, "gy": 2 * ph + lo}, device_id_type=MESH,
         )
 
-    def relay(i):
+    def relay(h, i):
+        cut = pl.ds(h * span, span)
         if isinstance(i, int) and i == 0:
-            src, at = mix_ref, modes_ref.at[gx, gy]
+            src, at = mix_ref.at[cut], modes_ref.at[gx, gy, cut]
         else:
             sx, sh = source(i)
-            src = at = modes_ref.at[sx, 2 * sh + lo]
+            src = at = modes_ref.at[sx, 2 * sh + lo, cut]
         return pltpu.make_async_remote_copy(
-            src_ref=src, dst_ref=at, send_sem=send4.at[i], recv_sem=recv4.at[i],
+            src_ref=src, dst_ref=at, send_sem=send4.at[h, i], recv_sem=recv4.at[h, i],
             device_id={"gy": mate}, device_id_type=MESH,
         )
 
@@ -193,25 +202,33 @@
                     eye, jnp.concatenate(parts, axis=0), (((1,), (1,)), ((), ())),
                     preferred_element_type=F32,
                 ).astype(BF)
-        pl.semaphore_wait(barrier, peers + n_col - 1)
-        for i in range(1, n_col):
-            share(i).start()
 
     def z_stage(u):
         h, s = units[u]
         field_copy(h, s).wait()
+        if u + 3 < len(units):
+            field_copy(*units[u + 3]).start()
         lhs = jnp.concatenate(
             [fields_ref[s * G + g, :, h * CH:(h + 1) * CH, :].reshape(yl * CH, Z) for g in range(G)],
             axis=-1,
         )
-        amp_ref[u % 2] = dot(lhs, depth_ref[...]).astype(BF)
+        value = dot(lhs, depth_ref[...]).reshape(yl, CH // CS, CS, 2 * G * MZ)
+        for e in range(CH // CS):
+            amp_ref[u % 2, e] = value[:, e].reshape(yl * CS, 2 * G * MZ).astype(BF)
 
     def y_stage(u):
         h, s = units[u]
         lanes = 2 * G * MZ
-        turn_ref[h % 2, :, s * lanes:(s + 1) * lanes] = dot(ky_ref[...], amp_ref[u % 2]).astype(BF)
-
-    piece = min(2, steps)
+        value = jnp.concatenate(
+            [
+                dot(ky_ref[...], amp_ref[u % 2, e]).reshape(2 * MY, CS, lanes)
+                for e in range(CH // CS)
+            ],
+            axis=1,
+        )
+        turn_ref[h % 2, :, s * lanes:(s + 1) * lanes] = value.reshape(2 * MY * CH, lanes).astype(BF)
+
+    piece = 1
 
     def x_stage(u):
         h, s = units[u]
@@ -242,17 +259,19 @@
                 send_ref[h, b, i] = value[:, b * L:(b + 1) * L]
         loop(1, peers, lambda i: scatter(h, i).start())
 
-    ready = min(2, len(units))
-    for u in range(len(units) + 2):
-        if u == ready:
-            prepare_weights()
+    for u in range(len(units) + 1):
         if u < len(units):
             z_stage(u)
-        if 0 <= u - 1 < len(units):
+        if u == 0:
+            prepare_weights()
+            pl.semaphore_wait(barrier, peers + n_col - 1)
+            for k in range(kyl):
+                for i in range(1, n_col):
+                    share(i, k).start()
+        if 0 <= u - 1:
             y_stage(u - 1)
-        if 0 <= u - 2:
-            x_stage(u - 2)
-        if halves > 1 and u == steps + 3:
+            x_stage(u - 1)
+        if halves > 1 and u == steps + 1:
             send_half(0)
 
     weight = skip_ref[...].astype(F32)
@@ -263,7 +282,8 @@
         wbd_ref[g * C:(g + 1) * C, :] = jnp.where(keep, tall, 0.0).astype(BF)
     diagonal = iota((C, C), 0) == iota((C, C), 1)
     bias = jnp.sum(jnp.where(diagonal, bias_ref[...], 0.0), 1, keepdims=True)
-    bias = (bias - jnp.mean(bias, axis=0, keepdims=True))[None]
+    gain = jnp.sum(jnp.where(diagonal, gain_ref[...], 0.0), 1, keepdims=True) * (0.5 ** 0.5)
+    bias = ((bias - jnp.mean(bias, axis=0, keepdims=True)) * gain)[None]
 
     def skip_cells(low, high):
         def go(i, carry):
@@ -272,20 +292,23 @@
                 hidden = jnp.concatenate(
                     [fields_ref[x + k, y:y + tile // C].reshape(tile, Z) for k in range(2)], axis=-1
                 )
-                part = dot(wbd_ref[...], hidden).reshape(tile // C, C, 2 * Z) + bias
+                part = dot(wbd_ref[...], hidden).reshape(tile // C, C, 2 * Z) * gain[None] + bias
                 for k in range(2):
                     pre_ref[x + k, y:y + tile // C] = part[:, :, k * Z:(k + 1) * Z]
             return carry
         lax.fori_loop(low, high, go, 0)
 
     pairs = xl // 2
-    skip_cells(0, pairs // 8)
+    early, mid = pairs // 8, pairs // 2
+    skip_cells(0, early)
     send_half(halves - 1)
 
     ti_ref[...] = spread_table(txi_ref[gx], 2 * xl * MZ, lambda j: div(j, MZ))
+    DS = 8 if per_dl(dl, n_col, halves) else CH
     th_ref[...] = spread_table(
-        tyi_ref[gy], 2 * MY * CH,
-        lambda j: div(j, per * kyl * dl) * kyl + mod(div(j, dl), kyl),
+        tyi_ref[gy], 2 * MY * DS,
+        (lambda j: div(j, DS)) if DS < CH else
+        (lambda j: div(j, per * kyl * dl) * kyl + mod(div(j, dl), kyl)),
     )
 
     def put_gx(first, value):
@@ -295,14 +318,12 @@
     band(put_gx, ti_ref, 4 * MX, MZ, iota((MZ, wide), 0) == mod(iota((MZ, wide), 1), MZ))
 
     def put_hy(first, value):
-        hy_ref[pl.ds(first, CH), :] = value
-
-    j = iota((CH, 2 * MY * CH), 1)
-    band(
-        put_hy, th_ref, yl, CH,
-        iota((CH, 2 * MY * CH), 0) == mod(div(j, kyl * dl), per) * dl + mod(j, dl),
-    )
-    skip_cells(pairs // 8, pairs // 2)
+        hy_ref[pl.ds(first, DS), :] = value
+
+    j = iota((DS, 2 * MY * DS), 1)
+    chan = mod(j, DS) if DS < CH else mod(div(j, kyl * dl), per) * dl + mod(j, dl)
+    band(put_hy, th_ref, yl, DS, iota((DS, 2 * MY * DS), 0) == chan)
+    skip_cells(early, early + mid)
 
     sums = {}
     for h in range(halves):
@@ -313,7 +334,8 @@
         spec = total.astype(BF).astype(F32)
         if h == 0:
             for i in range(1, n_col):
-                share(i).wait_recv()
+                for k in range(kyl):
+                    share(i, k).wait_recv()
         re, im = spec[:, :L // 2], spec[:, L // 2:]
         re = jnp.concatenate([re, re], axis=-1)
         im = jnp.concatenate([im, im], axis=-1)
@@ -335,29 +357,31 @@
         centre = sum(jnp.sum(m, axis=0, keepdims=True) for m in mixed) * (1.0 / C)
         for q in range(n_col):
             row = (q * kyl + k) * dl
-            mix_ref[row:row + dl] = (mixed[q] - centre).astype(BF)
-
-    loop(1, peers, lambda i: gather(i).start())
-    relay(0).start()
+            mix_ref[row:row + dl] = ((mixed[q] - centre) * gain[q * dl:(q + 1) * dl]).astype(BF)
+
+    for h in range(halves):
+        loop(1, peers, lambda i: gather(h, i).start())
+        relay(h, 0).start()
     modes_ref[gx, gy] = mix_ref[...]
-    skip_cells(pairs // 2, pairs)
-
-    def pass_on(i):
-        gather(i).wait_recv()
-        relay(i).start()
-
-    loop(1, peers, pass_on)
+    skip_cells(early + mid, pairs)
     for h in range(halves):
         swap(h).wait_send()
         loop(1, peers, lambda i: scatter(h, i).wait_send())
     for i in range(1, n_col):
-        share(i).wait_send()
-    relay(0).wait_recv()
-    loop(1, peers, lambda i: relay(i).wait_recv())
-
-    span = kyl * CH
+        for k in range(kyl):
+            share(i, k).wait_send()
+
     lanes = rows_ref.shape[-1]
     for h in range(halves):
+        def pass_on(i):
+            gather(h, i).wait_recv()
+            relay(h, i).start()
+
+        loop(1, peers, pass_on)
+
+    for h in range(halves):
+        relay(h, 0).wait_recv()
+        loop(1, peers, lambda i: relay(h, i).wait_recv())
         part = jnp.concatenate(
             [
                 jnp.concatenate([modes_ref[b, g, h * span:(h + 1) * span] for g in range(n_gy)], axis=0)
@@ -366,30 +390,46 @@
             axis=-1,
         )
         half = 2 * MX * MZ
+        wide = 2 * xl * MZ
         part = jnp.concatenate(
-            [dot(part, gx_ref[cs * half:(cs + 1) * half, :]).astype(BF) for cs in range(2)], axis=0
-        )
-        value = dot(hy_ref[...], part).astype(BF).reshape(yl, CH, 2 * xl * MZ)
+            [dot(part, gx_ref[cs * half:(cs + 1) * half, :]) for cs in range(2)], axis=0
+        ).reshape(2 * MY, CH // DS, DS, wide)
+        value = jnp.concatenate(
+            [
+                dot(hy_ref[...], part[:, e].reshape(2 * MY * DS, wide).astype(BF)).reshape(yl, DS, wide)
+                for e in range(CH // DS)
+            ],
+            axis=1,
+        ).astype(BF)
         for g in range(rows_ref.shape[0]):
             rows_ref[g, :, h * CH:(h + 1) * CH] = value[:, :, g * lanes:(g + 1) * lanes]
-    relay(0).wait_send()
-    loop(1, peers, lambda i: gather(i).wait_send())
-    loop(1, peers, lambda i: relay(i).wait_send())
-
-
-def back_kernel(sizes, rows_ref, pre_ref, depth_ref, gain_ref, shift_ref, out_hbm, out_ref, sem):
-    groups, G, yl, C, Z, cells = sizes
-
-    def column(ref):
-        return jnp.sum(jnp.where(iota((C, C), 0) == iota((C, C), 1), ref[...], 0.0), 1, keepdims=True)
+    for h in range(halves):
+        relay(h, 0).wait_send()
+        loop(1, peers, lambda i: gather(h, i).wait_send())
+        loop(1, peers, lambda i: relay(h, i).wait_send())
+
+
+def back_kernel(
+    sizes, rows_ref, pre_ref, depth_ref, gain_ref, shift_ref, out_hbm,
+    out_ref, part_ref, square_ref, weigh_ref, sem,
+):
+    trips, G, yl, C, Z, cells, unroll = sizes
+    tall, wide = cells * C, G * Z
 
     root = 0.5 ** 0.5
-    gain = (column(gain_ref) * root)[None]
-    shift = (column(shift_ref) * root)[None]
+    scale = gain_ref[...] * root
+    scale = 1.0 / (C * (scale * scale))
+    scale = jnp.concatenate([scale] * cells, axis=-1)
+    own = div(iota((8 * cells, tall), 0), 8) == div(iota((8 * cells, tall), 1), C)
+    weigh_ref[...] = jnp.where(own, scale, 0.0).astype(BF)
+    diagonal = iota((C, C), 0) == iota((C, C), 1)
+    shift = jnp.sum(jnp.where(diagonal, shift_ref[...], 0.0), 1, keepdims=True) * root
+    shift = jnp.broadcast_to(shift, (C, Z)).reshape(1, C // 8, 8, Z)
 
     def leave(i, slot):
+        at = i * unroll * G
         return pltpu.make_async_copy(
-            out_ref.at[slot], out_hbm.at[pl.ds(i * G, G)], sem.at[slot]
+            out_ref.at[slot], out_hbm.at[pl.ds(at, unroll * G)], sem.at[slot]
         )
 
     def go(i, carry):
@@ -399,19 +439,39 @@
         def _():
             leave(i - 2, slot).wait()
 
-        for y in range(0, yl, cells):
-            part = dot(rows_ref[i, y:y + cells].reshape(cells * C, rows_ref.shape[-1]), depth_ref[...])
+        tiles = [(a, y) for a in range(unroll) for y in range(0, yl, cells)]
+
+        def first(t):
+            a, y = tiles[t]
+            g = i * unroll + a
+            part = dot(rows_ref[g, y:y + cells].reshape(tall, rows_ref.shape[-1]), depth_ref[...])
             for k in range(G):
-                pre = part[:, k * Z:(k + 1) * Z].reshape(cells, C, Z) + pre_ref[i * G + k, y:y + cells]
-                spread = jnp.mean(pre * pre, axis=1, keepdims=True)
-                value = (pre * (lax.rsqrt(spread + norm_eps) * gain) + shift).astype(BF)
+                at = slice(k * Z, (k + 1) * Z)
+                value = part[:, at] + pre_ref[g * G + k, y:y + cells].reshape(tall, Z)
+                part_ref[t % 2, :, at] = value
+                square_ref[t % 2, :, at] = (value * value).astype(BF)
+
+        def second(t):
+            a, y = tiles[t]
+            spread = dot(weigh_ref[...], square_ref[t % 2])
+            spread = lax.rsqrt(spread + norm_eps).reshape(cells, 1, 8, wide)
+            for k in range(G):
+                at = slice(k * Z, (k + 1) * Z)
+                value = part_ref[t % 2, :, at].reshape(cells, C // 8, 8, Z)
+                value = (value * spread[..., at] + shift).reshape(cells, C, Z).astype(BF)
                 value = (value * root).astype(BF) * (1.0 + lax.erf(value)).astype(BF)
-                out_ref[slot, k, y:y + cells] = value
+                out_ref[slot, a * G + k, y:y + cells] = value
+
+        for t in range(len(tiles) + 1):
+            if t < len(tiles):
+                first(t)
+            if t >= 1:
+                second(t - 1)
         leave(i, slot).start()
         return carry
 
-    lax.fori_loop(0, groups, go, 0)
-    for i in range(max(0, groups - 2), groups):
+    lax.fori_loop(0, trips, go, 0)
+    for i in range(max(0, trips - 2), trips):
         leave(i, i % 2).wait()
 
 
@@ -458,6 +518,8 @@
 
         halves = 2 if C % 32 == 0 and n_col % 2 == 0 else 1
         CH = C // halves
+        CS = 8 if CH % 8 == 0 else CH
+        DS = 8 if per_dl(dl, n_col, halves) else CH
         turned = jnp.transpose(weights, (0, 1, 2, 4, 5, 3))
         tile = min(256, yl * C)
 
@@ -471,13 +533,13 @@
                 pltpu.VMEM((xl // G2, yl, C, G2 * 2 * MZ), BF),
                 pltpu.VMEM((xl, yl, C, Z), F32),
             ),
-            in_specs=[outside, outside] + [inside] * (len(tables) + 2),
+            in_specs=[outside, outside] + [inside] * (len(tables) + 3),
             out_specs=(inside, inside),
             scratch_shapes=[
                 pltpu.VMEM((xl, yl, C, Z), BF),
-                pltpu.VMEM((2 * MY * CH, yl * CH), BF),
+                pltpu.VMEM((2 * MY * CS, yl * CS), BF),
                 pltpu.VMEM((4 * xl * MZ, 2 * MX * MZ), BF),
-                pltpu.VMEM((2, yl * CH, G * 2 * MZ), BF),
+                pltpu.VMEM((2, CH // CS, yl * CS, G * 2 * MZ), BF),
                 pltpu.VMEM((2, 2 * MY * CH, xl * 2 * MZ), BF),
                 pltpu.VMEM((2, MY * CH, 2 * MX * MZ), F32),
                 pltpu.VMEM((halves, n_hi, kyl * CH, n_gx * L), BF),
@@ -487,42 +549,46 @@
                 pltpu.VMEM((kyl * C, L), BF),
                 pltpu.VMEM((n_gx, n_gy, kyl * C, L), BF),
                 pltpu.VMEM((4 * MX * MZ, 2 * xl * MZ), BF),
-                pltpu.VMEM((yl * CH, 2 * MY * CH), BF),
+                pltpu.VMEM((yl * DS, 2 * MY * DS), BF),
                 pltpu.VMEM(turned.shape, BF),
                 pltpu.VMEM((n_col, kyl, dl, C, L), BF),
                 pltpu.VMEM((tile, tile), BF),
-                pltpu.VMEM((2 * MY, yl * CH), F32),
+                pltpu.VMEM((2 * MY, yl * CS), F32),
                 pltpu.VMEM((4 * xl, 2 * MX * MZ), F32),
                 pltpu.VMEM((4 * MX, 2 * xl * MZ), F32),
-                pltpu.VMEM((yl, 2 * MY * CH), F32),
+                pltpu.VMEM((yl, 2 * MY * DS), F32),
                 pltpu.SemaphoreType.DMA((halves, steps)),
                 pltpu.SemaphoreType.DMA,
                 pltpu.SemaphoreType.DMA((halves,)),
                 pltpu.SemaphoreType.DMA((halves,)),
                 pltpu.SemaphoreType.DMA((halves, peers)),
                 pltpu.SemaphoreType.DMA((halves, peers)),
-                pltpu.SemaphoreType.DMA((n_col,)),
-                pltpu.SemaphoreType.DMA((n_col,)),
-                pltpu.SemaphoreType.DMA((peers,)),
-                pltpu.SemaphoreType.DMA((peers,)),
-                pltpu.SemaphoreType.DMA((peers,)),
-                pltpu.SemaphoreType.DMA((peers,)),
+                pltpu.SemaphoreType.DMA((n_col, kyl)),
+                pltpu.SemaphoreType.DMA((n_col, kyl)),
+                pltpu.SemaphoreType.DMA((halves, peers)),
+                pltpu.SemaphoreType.DMA((halves, peers)),
+                pltpu.SemaphoreType.DMA((halves, peers)),
+                pltpu.SemaphoreType.DMA((halves, peers)),
             ],
             compiler_params=pltpu.CompilerParams(
                 collective_id=0, has_side_effects=True, vmem_limit_bytes=40 * 2**20,
             ),
             name="front",
-        )(hidden, turned, *tables, skip_weight[0], skip_bias)
+        )(hidden, turned, *tables, skip_weight[0], skip_bias, norm_gain)
 
         groups = xl // G2
         cells = min(8, yl)
+        unroll = 1 if groups % 1 == 0 else 1
         out = pl.pallas_call(
-            functools.partial(back_kernel, (groups, G2, yl, C, Z, cells)),
+            functools.partial(back_kernel, (groups // unroll, G2, yl, C, Z, cells, unroll)),
             out_shape=jax.ShapeDtypeStruct(hidden.shape, BF),
             in_specs=[inside] * 5,
             out_specs=outside,
             scratch_shapes=[
-                pltpu.VMEM((2, G2, yl, C, Z), BF),
+                pltpu.VMEM((2, unroll * G2, yl, C, Z), BF),
+                pltpu.VMEM((2, cells * C, G2 * Z), F32),
+                pltpu.VMEM((2, cells * C, G2 * Z), BF),
+                pltpu.VMEM((8 * cells, cells * C), BF),
                 pltpu.SemaphoreType.DMA((2,)),
             ],
             compiler_params=pltpu.CompilerParams(vmem_limit_bytes=12 * 2**20),

time: 45.6 us -> 43.5 us (0.954)
  Pallas kernels: 45.5 us -> 43 us
    pallas_call x1, Pallas kernels: 34.7 us -> 32.7 us  [local(): pl.pallas_call(functools.partial(front_kernel, sizes), out_shape=(pltpu.V...]
    pallas_call x1, Pallas kernels: 10.8 us -> 10.3 us  [local(): pl.pallas_call(functools.partial(back_kernel, (groups // unroll, G2, yl,...]
where the time goes in v2:
time: 43.5 us; the launch traced here: 43 us
  Pallas kernels  43 us (99%)
    pallas_call x1, Pallas kernels, local(): pl.pallas_call(functools.partial(front_kernel, sizes), out_shape=(pltpu.V...  32.7 us
    pallas_call x1, Pallas kernels, local(): pl.pallas_call(functools.partial(back_kernel, (groups // unroll, G2, yl,...  10.3 us

profile of v2, /device:TPU:1, one launch (start us, length us, event | category | flops | bytes accessed | tf_op | source)
XLA Modules:
  0.0 43.0 jit_solution(15353157471497525224)
XLA Ops:
  0.0 0.0 copy-start
  0.0 0.0 copy-start.1
  0.0 0.0 copy-start.2
  0.0 32.7 %front.1 = (bf16[8,32,32,128]{3,2,1,0:T(8,128)(2,1)S(1)}, f32[32,32,32,128]{3,2,1,0:T(8,128)S(1)}) custom-call(bf16[32,32,32,128]{3,2,1,0:T(8,128)(2,1)} %bitcast.6, bf16[4,4,2,16,16,32]{5,4,3,2,1,0:T(8,128)(2,1)} %bitcast.7, bf16[1024,256]{1,0:T(8,128)(2,1)} %constant.19.depth_ref, bf16[4,32,32]{2,1,0:T(8,128)(2,1)} %constant.20.tyf_ref, ...), custom_call_target="tpu_custom_call" | custom-call | tf_op jit(solution)/shard_map/front/pallas_call | solution.py:530
  32.7 0.0 copy-done
  32.7 0.0 copy-done.1
  32.7 0.0 copy-done.2
  32.7 10.3 %back.1 = bf16[32,32,32,128]{3,2,1,0:T(8,128)(2,1)} custom-call(bf16[8,32,32,128]{3,2,1,0:T(8,128)(2,1)S(1)} %get-tuple-element.7.rows_ref, f32[32,32,32,128]{3,2,1,0:T(8,128)S(1)} %get-tuple-element.8.pre_ref, bf16[128,512]{1,0:T(8,128)(2,1)S(1)} %copy-done, f32[1,32]{1,0:T(1,128)S(1)} %copy-done.1, f32[1,32]{1,0:T(1,128)S(1)} %copy-done.2), custom_call_target="tpu_custom_call" | custom-call | tf_op jit(solution)/shard_map/back/pallas_call | solution.py:582
Async XLA Ops:
  0.0 32.7 %copy-start = (bf16[128,512]{1,0:T(8,128)(2,1)S(1)}, bf16[128,512]{1,0:T(8,128)(2,1)}, u32[]{:S(2)}) copy-start(bf16[128,512]{1,0:T(8,128)(2,1)} %constant.24.depth_ref) | copy-start | bytes 393220
  0.0 32.7 %copy-start.1 = (f32[1,32]{1,0:T(1,128)S(1)}, f32[1,32]{1,0:T(1,128)}, u32[]{:S(2)}) copy-start(f32[1,32]{1,0:T(1,128)} %gain_ref.3) | copy-start | bytes 388
  0.0 32.7 %copy-start.2 = (f32[1,32]{1,0:T(1,128)S(1)}, f32[1,32]{1,0:T(1,128)}, u32[]{:S(2)}) copy-start(f32[1,32]{1,0:T(1,128)} %shift_ref.1) | copy-start | bytes 388

commit v3 on v2

--- a/solution.py
+++ b/solution.py
@@ -53,6 +53,11 @@
     return dot(table, right)
 
 
+def columns(rows, width):
+    tile = 256 if width % 256 == 0 else width
+    return (width // tile, rows, tile)
+
+
 def per_dl(dl, n_col, halves):
     return n_col == halves and dl % 8 == 0
 
@@ -64,12 +69,14 @@
 
 def front_kernel(
     sizes,
-    fields_hbm, spectral_hbm, depth_ref, tyf_ref, txf_ref, txi_ref, tyi_ref, skip_ref, bias_ref, gain_ref,
+    fields_hbm, spectral_hbm,
+    depth_hbm, tyf_hbm, txf_hbm, txi_hbm, tyi_hbm, skip_hbm, bias_hbm, gain_hbm,
     rows_ref, pre_ref,
     fields_ref, ky_ref, kx_ref, amp_ref, turn_ref, total_ref,
     swap_ref, take_ref, send_ref, recv_ref, mix_ref, modes_ref, gx_ref, hy_ref, w_ref, wa_ref,
     wbd_ref, ty_ref, tx_ref, ti_ref, th_ref,
     fsem, wsem, swap_s, swap_r, send1, recv1, send2, recv2, send3, recv3, send4, recv4,
+    depth_ref, tyf_ref, txf_ref, txi_ref, tyi_ref, skip_ref, bias_ref, gain_ref, gcol_ref, tsem,
 ):
     n_gx, n_gy, n_col, xl, yl, C, MY, MZ, kxl, kyl, dl, G, steps, halves, tile = sizes
     n_hi = n_gy // 2
@@ -113,10 +120,22 @@
 
     weights_copy = pltpu.make_async_copy(spectral_hbm, w_ref, wsem)
     units = [(h, s) for h in range(halves) for s in range(steps)]
-    field_copy(*units[0]).start()
+    small = [
+        pltpu.make_async_copy(src, dst, tsem.at[n])
+        for n, (src, dst) in enumerate((
+            (tyf_hbm.at[gy], tyf_ref), (txf_hbm.at[gx], txf_ref), (depth_hbm, depth_ref),
+            (txi_hbm.at[gx], txi_ref), (tyi_hbm.at[gy], tyi_ref), (skip_hbm, skip_ref),
+            (bias_hbm, bias_ref), (gain_hbm, gain_ref),
+        ))
+    ]
+    for copy in small[:2]:
+        copy.start()
     weights_copy.start()
-    for unit in units[1:3]:
+    small[2].start()
+    for unit in units[:3]:
         field_copy(*unit).start()
+    for copy in small[3:]:
+        copy.start()
 
     barrier = pltpu.get_barrier_semaphore()
 
@@ -133,8 +152,10 @@
     loop(1, n_col, greet_side)
     pl.semaphore_signal(barrier, inc=1, device_id={"gy": mate}, device_id_type=MESH)
 
-    ty_ref[...] = spread_table(tyf_ref[gy], yl * CS, lambda j: div(j, CS))
-    tx_ref[...] = spread_table(txf_ref[gx], 2 * MX * MZ, lambda j: div(j, MZ))
+    for copy in small[:2]:
+        copy.wait()
+    ty_ref[...] = spread_table(tyf_ref[...], yl * CS, lambda j: div(j, CS))
+    tx_ref[...] = spread_table(txf_ref[...], 2 * MX * MZ, lambda j: div(j, MZ))
 
     def put_ky(first, value):
         ky_ref[pl.ds(first, CS), :] = value
@@ -142,7 +163,8 @@
     band(put_ky, ty_ref, 2 * MY, CS, iota((CS, yl * CS), 0) == mod(iota((CS, yl * CS), 1), CS))
 
     def put_kx(first, value):
-        kx_ref[pl.ds(first, MZ), :] = value
+        for n in range(kx_ref.shape[0]):
+            kx_ref[n, pl.ds(first, MZ), :] = value[:, n * kx_ref.shape[2]:(n + 1) * kx_ref.shape[2]]
 
     wide = 2 * MX * MZ
     band(put_kx, tx_ref, 4 * steps * G, MZ, iota((MZ, wide), 0) == mod(iota((MZ, wide), 1), MZ))
@@ -170,10 +192,11 @@
         )
 
     span = kyl * C // halves
+    each = n_col // halves
 
     def gather(h, i):
         px, ph = peer(i)
-        cut = pl.ds(h * span, span)
+        cut = pl.ds(h * each, each)
         return pltpu.make_async_remote_copy(
             src_ref=mix_ref.at[cut], dst_ref=modes_ref.at[gx, gy, cut],
             send_sem=send3.at[h, i], recv_sem=recv3.at[h, i],
@@ -181,7 +204,7 @@
         )
 
     def relay(h, i):
-        cut = pl.ds(h * span, span)
+        cut = pl.ds(h * each, each)
         if isinstance(i, int) and i == 0:
             src, at = mix_ref.at[cut], modes_ref.at[gx, gy, cut]
         else:
@@ -202,6 +225,10 @@
                     eye, jnp.concatenate(parts, axis=0), (((1,), (1,)), ((), ())),
                     preferred_element_type=F32,
                 ).astype(BF)
+            if k == 0:
+                pl.semaphore_wait(barrier, peers + n_col - 1)
+            for i in range(1, n_col):
+                share(i, k).start()
 
     def z_stage(u):
         h, s = units[u]
@@ -212,9 +239,14 @@
             [fields_ref[s * G + g, :, h * CH:(h + 1) * CH, :].reshape(yl * CH, Z) for g in range(G)],
             axis=-1,
         )
-        value = dot(lhs, depth_ref[...]).reshape(yl, CH // CS, CS, 2 * G * MZ)
-        for e in range(CH // CS):
-            amp_ref[u % 2, e] = value[:, e].reshape(yl * CS, 2 * G * MZ).astype(BF)
+        rows = yl // 2
+        for f in range(2):
+            value = dot(lhs[f * rows * CH:(f + 1) * rows * CH], depth_ref[...])
+            value = value.reshape(rows, CH // CS, CS, 2 * G * MZ)
+            for e in range(CH // CS):
+                amp_ref[u % 2, e, f * rows * CS:(f + 1) * rows * CS] = value[:, e].reshape(
+                    rows * CS, 2 * G * MZ
+                ).astype(BF)
 
     def y_stage(u):
         h, s = units[u]
@@ -226,54 +258,51 @@
             ],
             axis=1,
         )
-        turn_ref[h % 2, :, s * lanes:(s + 1) * lanes] = value.reshape(2 * MY * CH, lanes).astype(BF)
-
-    piece = 1
+        turn_ref[h % 2, s] = value.reshape(2 * MY * CH, lanes).astype(BF)
+
+    def joined(ref, low, high):
+        return jnp.concatenate([ref[n, low:high] for n in range(ref.shape[0])], axis=-1)
 
     def x_stage(u):
         h, s = units[u]
-        if s % piece != piece - 1:
-            return
-        lanes = piece * 2 * G * MZ
-        cut = slice((s + 1) * 2 * G * MZ - lanes, (s + 1) * 2 * G * MZ)
-        count = steps * 2 * G * MZ
-        term = dot(turn_ref[h % 2, :top, cut], kx_ref[cut.start:cut.stop, :])
-        term = term + dot(turn_ref[h % 2, top:, cut], kx_ref[count + cut.start:count + cut.stop, :])
-        if s == piece - 1:
-            total_ref[h % 2] = term
-        else:
-            total_ref[h % 2] += term
+        lanes = 2 * G * MZ
+        term = dot(turn_ref[h % 2, s, :top], joined(kx_ref, s * lanes, (s + 1) * lanes))
+        later = (steps + s) * lanes
+        term = term + dot(turn_ref[h % 2, s, top:], joined(kx_ref, later, later + lanes))
+        for b in range(n_gx):
+            if s == 0:
+                total_ref[h % 2, b] = term[:, b * L:(b + 1) * L]
+            else:
+                total_ref[h % 2, b] += term[:, b * L:(b + 1) * L]
         if s == steps - 1:
             for i in range(n_hi):
                 at = pl.multiple_of((2 * i + 1 - lo) * block, block)
-                swap_ref[h, i] = total_ref[h % 2, pl.ds(at, block), :].astype(BF)
+                for b in range(n_gx):
+                    swap_ref[h, i, b] = total_ref[h % 2, b, pl.ds(at, block), :].astype(BF)
             swap(h).start()
 
     def send_half(h):
         swap(h).wait_recv()
         for i in range(n_hi):
             at = pl.multiple_of((2 * i + lo) * block, block)
-            value = total_ref[h % 2, pl.ds(at, block), :] + take_ref[h, i].astype(F32)
-            value = value.astype(BF)
             for b in range(n_gx):
-                send_ref[h, b, i] = value[:, b * L:(b + 1) * L]
+                value = total_ref[h % 2, b, pl.ds(at, block), :] + take_ref[h, i, b].astype(F32)
+                send_ref[h, b, i] = value.astype(BF)
         loop(1, peers, lambda i: scatter(h, i).start())
 
+    prepare_weights()
+    small[2].wait()
     for u in range(len(units) + 1):
         if u < len(units):
             z_stage(u)
-        if u == 0:
-            prepare_weights()
-            pl.semaphore_wait(barrier, peers + n_col - 1)
-            for k in range(kyl):
-                for i in range(1, n_col):
-                    share(i, k).start()
         if 0 <= u - 1:
             y_stage(u - 1)
             x_stage(u - 1)
         if halves > 1 and u == steps + 1:
             send_half(0)
 
+    for copy in small[3:]:
+        copy.wait()
     weight = skip_ref[...].astype(F32)
     weight = (weight - jnp.mean(weight, axis=0, keepdims=True)).astype(BF)
     tall = spread_table(weight, tile, lambda j: mod(j, C))
@@ -283,6 +312,8 @@
     diagonal = iota((C, C), 0) == iota((C, C), 1)
     bias = jnp.sum(jnp.where(diagonal, bias_ref[...], 0.0), 1, keepdims=True)
     gain = jnp.sum(jnp.where(diagonal, gain_ref[...], 0.0), 1, keepdims=True) * (0.5 ** 0.5)
+    for q in range(n_col):
+        gcol_ref[q] = jnp.broadcast_to(gain[q * dl:(q + 1) * dl], (dl, L))
     bias = ((bias - jnp.mean(bias, axis=0, keepdims=True)) * gain)[None]
 
     def skip_cells(low, high):
@@ -303,16 +334,17 @@
     skip_cells(0, early)
     send_half(halves - 1)
 
-    ti_ref[...] = spread_table(txi_ref[gx], 2 * xl * MZ, lambda j: div(j, MZ))
+    ti_ref[...] = spread_table(txi_ref[...], 2 * xl * MZ, lambda j: div(j, MZ))
     DS = 8 if per_dl(dl, n_col, halves) else CH
     th_ref[...] = spread_table(
-        tyi_ref[gy], 2 * MY * DS,
+        tyi_ref[...], 2 * MY * DS,
         (lambda j: div(j, DS)) if DS < CH else
         (lambda j: div(j, per * kyl * dl) * kyl + mod(div(j, dl), kyl)),
     )
 
     def put_gx(first, value):
-        gx_ref[pl.ds(first, MZ), :] = value
+        for n in range(gx_ref.shape[0]):
+            gx_ref[n, pl.ds(first, MZ), :] = value[:, n * gx_ref.shape[2]:(n + 1) * gx_ref.shape[2]]
 
     wide = 2 * xl * MZ
     band(put_gx, ti_ref, 4 * MX, MZ, iota((MZ, wide), 0) == mod(iota((MZ, wide), 1), MZ))
@@ -332,38 +364,44 @@
             scatter(h, i).wait_recv()
             total = total + recv_ref[h, i].astype(F32)
         spec = total.astype(BF).astype(F32)
-        if h == 0:
-            for i in range(1, n_col):
-                for k in range(kyl):
-                    share(i, k).wait_recv()
         re, im = spec[:, :L // 2], spec[:, L // 2:]
         re = jnp.concatenate([re, re], axis=-1)
         im = jnp.concatenate([im, im], axis=-1)
-        for q in range(n_col):
+        for a in range(n_col):
             for k in range(kyl):
+                if h == 0 and a > 0:
+                    share(n_col - a, k).wait_recv()
                 rows, chans = slice(k * CH, (k + 1) * CH), slice(h * CH, (h + 1) * CH)
-                weight = wa_ref[q, k, :, chans].astype(F32)
+                weight = wa_ref[side(a), k, :, chans].astype(F32)
                 new = [jnp.sum(v[rows][None] * weight, axis=1) for v in (re, im)]
-                old = sums.get((q, k))
-                sums[q, k] = new if old is None else [a + b for a, b in zip(old, new)]
+                old = sums.get((a, k))
+                sums[a, k] = new if old is None else [x + y for x, y in zip(old, new)]
     for k in range(kyl):
         mixed = []
-        for q in range(n_col):
-            first, second = sums[q, k]
+        for a in range(n_col):
+            first, second = sums[a, k]
             turned_second = jnp.concatenate(
                 [-second[:, L // 2:], second[:, :L // 2]], axis=-1
             )
             mixed.append(first + turned_second)
         centre = sum(jnp.sum(m, axis=0, keepdims=True) for m in mixed) * (1.0 / C)
-        for q in range(n_col):
-            row = (q * kyl + k) * dl
-            mix_ref[row:row + dl] = ((mixed[q] - centre) * gain[q * dl:(q + 1) * dl]).astype(BF)
-
-    for h in range(halves):
+        for a in range(n_col):
+            mix_ref[side(a), k] = ((mixed[a] - centre) * gcol_ref[side(a)]).astype(BF)
+
+    def send_modes(h):
         loop(1, peers, lambda i: gather(h, i).start())
         relay(h, 0).start()
+
+    def sent_modes(h):
+        loop(1, peers, lambda i: gather(h, i).wait_send())
+        relay(h, 0).wait_send()
+
+    send_modes(0)
     modes_ref[gx, gy] = mix_ref[...]
     skip_cells(early + mid, pairs)
+    for h in range(1, halves):
+        sent_modes(h - 1)
+        send_modes(h)
     for h in range(halves):
         swap(h).wait_send()
         loop(1, peers, lambda i: scatter(h, i).wait_send())
@@ -378,13 +416,11 @@
             relay(h, i).start()
 
         loop(1, peers, pass_on)
-
-    for h in range(halves):
         relay(h, 0).wait_recv()
         loop(1, peers, lambda i: relay(h, i).wait_recv())
         part = jnp.concatenate(
             [
-                jnp.concatenate([modes_ref[b, g, h * span:(h + 1) * span] for g in range(n_gy)], axis=0)
+                jnp.concatenate([modes_ref[b, g, h * each:(h + 1) * each].reshape(span, L) for g in range(n_gy)], axis=0)
                 for b in range(n_gx)
             ],
             axis=-1,
@@ -392,7 +428,7 @@
         half = 2 * MX * MZ
         wide = 2 * xl * MZ
         part = jnp.concatenate(
-            [dot(part, gx_ref[cs * half:(cs + 1) * half, :]) for cs in range(2)], axis=0
+            [dot(part, joined(gx_ref, cs * half, (cs + 1) * half)) for cs in range(2)], axis=0
         ).reshape(2 * MY, CH // DS, DS, wide)
         value = jnp.concatenate(
             [
@@ -403,9 +439,8 @@
         ).astype(BF)
         for g in range(rows_ref.shape[0]):
             rows_ref[g, :, h * CH:(h + 1) * CH] = value[:, :, g * lanes:(g + 1) * lanes]
+    sent_modes(halves - 1)
     for h in range(halves):
-        relay(h, 0).wait_send()
-        loop(1, peers, lambda i: gather(h, i).wait_send())
         loop(1, peers, lambda i: relay(h, i).wait_send())
 
 
@@ -448,16 +483,17 @@
             for k in range(G):
                 at = slice(k * Z, (k + 1) * Z)
                 value = part[:, at] + pre_ref[g * G + k, y:y + cells].reshape(tall, Z)
-                part_ref[t % 2, :, at] = value
-                square_ref[t % 2, :, at] = (value * value).astype(BF)
+                part_ref[t % 2, k] = value
+                square_ref[t % 2, k] = (value * value).astype(BF)
 
         def second(t):
             a, y = tiles[t]
-            spread = dot(weigh_ref[...], square_ref[t % 2])
+            square = jnp.concatenate([square_ref[t % 2, k] for k in range(G)], axis=-1)
+            spread = dot(weigh_ref[...], square)
             spread = lax.rsqrt(spread + norm_eps).reshape(cells, 1, 8, wide)
             for k in range(G):
                 at = slice(k * Z, (k + 1) * Z)
-                value = part_ref[t % 2, :, at].reshape(cells, C // 8, 8, Z)
+                value = part_ref[t % 2, k].reshape(cells, C // 8, 8, Z)
                 value = (value * spread[..., at] + shift).reshape(cells, C, Z).astype(BF)
                 value = (value * root).astype(BF) * (1.0 + lax.erf(value)).astype(BF)
                 out_ref[slot, a * G + k, y:y + cells] = value
@@ -533,22 +569,22 @@
                 pltpu.VMEM((xl // G2, yl, C, G2 * 2 * MZ), BF),
                 pltpu.VMEM((xl, yl, C, Z), F32),
             ),
-            in_specs=[outside, outside] + [inside] * (len(tables) + 3),
+            in_specs=[outside] * (len(tables) + 5),
             out_specs=(inside, inside),
             scratch_shapes=[
                 pltpu.VMEM((xl, yl, C, Z), BF),
                 pltpu.VMEM((2 * MY * CS, yl * CS), BF),
-                pltpu.VMEM((4 * xl * MZ, 2 * MX * MZ), BF),
+                pltpu.VMEM(columns(4 * xl * MZ, 2 * MX * MZ), BF),
                 pltpu.VMEM((2, CH // CS, yl * CS, G * 2 * MZ), BF),
-                pltpu.VMEM((2, 2 * MY * CH, xl * 2 * MZ), BF),
-                pltpu.VMEM((2, MY * CH, 2 * MX * MZ), F32),
-                pltpu.VMEM((halves, n_hi, kyl * CH, n_gx * L), BF),
-                pltpu.VMEM((halves, n_hi, kyl * CH, n_gx * L), BF),
+                pltpu.VMEM((2, steps, 2 * MY * CH, G * 2 * MZ), BF),
+                pltpu.VMEM((2, n_gx, MY * CH, L), F32),
+                pltpu.VMEM((halves, n_hi, n_gx, kyl * CH, L), BF),
+                pltpu.VMEM((halves, n_hi, n_gx, kyl * CH, L), BF),
                 pltpu.VMEM((halves, n_gx, n_hi, kyl * CH, L), BF),
                 pltpu.VMEM((halves, peers, kyl * CH, L), BF),
-                pltpu.VMEM((kyl * C, L), BF),
-                pltpu.VMEM((n_gx, n_gy, kyl * C, L), BF),
-                pltpu.VMEM((4 * MX * MZ, 2 * xl * MZ), BF),
+                pltpu.VMEM((n_col, kyl, dl, L), BF),
+                pltpu.VMEM((n_gx, n_gy, n_col, kyl, dl, L), BF),
+                pltpu.VMEM(columns(4 * MX * MZ, 2 * xl * MZ), BF),
                 pltpu.VMEM((yl * DS, 2 * MY * DS), BF),
                 pltpu.VMEM(turned.shape, BF),
                 pltpu.VMEM((n_col, kyl, dl, C, L), BF),
@@ -569,6 +605,16 @@
                 pltpu.SemaphoreType.DMA((halves, peers)),
                 pltpu.SemaphoreType.DMA((halves, peers)),
                 pltpu.SemaphoreType.DMA((halves, peers)),
+                pltpu.VMEM(tables[0].shape, BF),
+                pltpu.VMEM(tables[1].shape[1:], BF),
+                pltpu.VMEM(tables[2].shape[1:], BF),
+                pltpu.VMEM(tables[3].shape[1:], BF),
+                pltpu.VMEM(tables[4].shape[1:], BF),
+                pltpu.VMEM((C, C), BF),
+                pltpu.VMEM((1, C), F32),
+                pltpu.VMEM((1, C), F32),
+                pltpu.VMEM((n_col, dl, L), F32),
+                pltpu.SemaphoreType.DMA((8,)),
             ],
             compiler_params=pltpu.CompilerParams(
                 collective_id=0, has_side_effects=True, vmem_limit_bytes=40 * 2**20,
@@ -586,8 +632,8 @@
             out_specs=outside,
             scratch_shapes=[
                 pltpu.VMEM((2, unroll * G2, yl, C, Z), BF),
-                pltpu.VMEM((2, cells * C, G2 * Z), F32),
-                pltpu.VMEM((2, cells * C, G2 * Z), BF),
+                pltpu.VMEM((2, G2, cells * C, Z), F32),
+                pltpu.VMEM((2, G2, cells * C, Z), BF),
                 pltpu.VMEM((8 * cells, cells * C), BF),
                 pltpu.SemaphoreType.DMA((2,)),
             ],

time: 43.5 us -> 41.5 us (0.954)
  Pallas kernels: 43 us -> 41.3 us
    pallas_call x1, Pallas kernels: 32.7 us -> 31.1 us  [local(): pl.pallas_call(functools.partial(front_kernel, sizes), out_shape=(pltpu.V...]
where the time goes in v3:
time: 41.5 us; the launch traced here: 41.3 us
  Pallas kernels  41.3 us (100%)
    pallas_call x1, Pallas kernels, local(): pl.pallas_call(functools.partial(front_kernel, sizes), out_shape=(pltpu.V...  31.1 us
    pallas_call x1, Pallas kernels, local(): pl.pallas_call(functools.partial(back_kernel, (groups // unroll, G2, yl,...  10.2 us

profile of v3, /device:TPU:1, one launch (start us, length us, event | category | flops | bytes accessed | tf_op | source)
XLA Modules:
  0.0 41.3 jit_solution(10492030155652290536)
XLA Ops:
  0.0 0.0 copy-start
  0.0 0.0 copy-start.1
  0.0 0.0 copy-start.2
  0.0 31.1 %front.1 = (bf16[8,32,32,128]{3,2,1,0:T(8,128)(2,1)S(1)}, f32[32,32,32,128]{3,2,1,0:T(8,128)S(1)}) custom-call(bf16[32,32,32,128]{3,2,1,0:T(8,128)(2,1)} %bitcast.6, bf16[4,4,2,16,16,32]{5,4,3,2,1,0:T(8,128)(2,1)} %bitcast.7, bf16[1024,256]{1,0:T(8,128)(2,1)} %constant.19.depth_hbm, bf16[4,32,32]{2,1,0:T(8,128)(2,1)} %constant.20.tyf_hbm, ...), custom_call_target="tpu_custom_call" | custom-call | tf_op jit(solution)/shard_map/front/pallas_call | solution.py:566
  31.1 0.0 copy-done
  31.1 0.0 copy-done.1
  31.1 0.0 copy-done.2
  31.2 10.2 %back.1 = bf16[32,32,32,128]{3,2,1,0:T(8,128)(2,1)} custom-call(bf16[8,32,32,128]{3,2,1,0:T(8,128)(2,1)S(1)} %get-tuple-element.7.rows_ref, f32[32,32,32,128]{3,2,1,0:T(8,128)S(1)} %get-tuple-element.8.pre_ref, bf16[128,512]{1,0:T(8,128)(2,1)S(1)} %copy-done, f32[1,32]{1,0:T(1,128)S(1)} %copy-done.1, f32[1,32]{1,0:T(1,128)S(1)} %copy-done.2), custom_call_target="tpu_custom_call" | custom-call | tf_op jit(solution)/shard_map/back/pallas_call | solution.py:628
Async XLA Ops:
  0.0 31.1 %copy-start = (bf16[128,512]{1,0:T(8,128)(2,1)S(1)}, bf16[128,512]{1,0:T(8,128)(2,1)}, u32[]{:S(2)}) copy-start(bf16[128,512]{1,0:T(8,128)(2,1)} %constant.24.depth_ref) | copy-start | bytes 393220
  0.0 31.1 %copy-start.1 = (f32[1,32]{1,0:T(1,128)S(1)}, f32[1,32]{1,0:T(1,128)}, u32[]{:S(2)}) copy-start(f32[1,32]{1,0:T(1,128)} %gain_ref.1) | copy-start | bytes 388
  0.0 31.1 %copy-start.2 = (f32[1,32]{1,0:T(1,128)S(1)}, f32[1,32]{1,0:T(1,128)}, u32[]{:S(2)}) copy-start(f32[1,32]{1,0:T(1,128)} %shift_ref.1) | copy-start | bytes 388

commit v4 on v3

--- a/solution.py
+++ b/solution.py
@@ -446,25 +446,25 @@
 
 def back_kernel(
     sizes, rows_ref, pre_ref, depth_ref, gain_ref, shift_ref, out_hbm,
-    out_ref, part_ref, square_ref, weigh_ref, sem,
+    out_ref, part_ref, square_ref, sem,
 ):
     trips, G, yl, C, Z, cells, unroll = sizes
     tall, wide = cells * C, G * Z
 
     root = 0.5 ** 0.5
-    scale = gain_ref[...] * root
-    scale = 1.0 / (C * (scale * scale))
-    scale = jnp.concatenate([scale] * cells, axis=-1)
-    own = div(iota((8 * cells, tall), 0), 8) == div(iota((8 * cells, tall), 1), C)
-    weigh_ref[...] = jnp.where(own, scale, 0.0).astype(BF)
     diagonal = iota((C, C), 0) == iota((C, C), 1)
     shift = jnp.sum(jnp.where(diagonal, shift_ref[...], 0.0), 1, keepdims=True) * root
     shift = jnp.broadcast_to(shift, (C, Z)).reshape(1, C // 8, 8, Z)
-
-    def leave(i, slot):
-        at = i * unroll * G
+    inverse = 1.0 / (jnp.sum(jnp.where(diagonal, gain_ref[...], 0.0), 1, keepdims=True) * root)
+    inverse = jnp.broadcast_to(inverse, (C, Z)).reshape(1, C // 8, 8, Z)
+
+    tiles = [(a, y) for a in range(unroll) for y in range(0, yl, cells)]
+
+    def leave(i, slot, t):
+        a, y = tiles[t]
         return pltpu.make_async_copy(
-            out_ref.at[slot], out_hbm.at[pl.ds(at, unroll * G)], sem.at[slot]
+            out_ref.at[slot, pl.ds(a * G, G), pl.ds(y, cells)],
+            out_hbm.at[pl.ds((i * unroll + a) * G, G), pl.ds(y, cells)], sem.at[slot, t],
         )
 
     def go(i, carry):
@@ -472,9 +472,8 @@
 
         @pl.when(i >= 2)
         def _():
-            leave(i - 2, slot).wait()
-
-        tiles = [(a, y) for a in range(unroll) for y in range(0, yl, cells)]
+            for t in range(len(tiles)):
+                leave(i - 2, slot, t).wait()
 
         def first(t):
             a, y = tiles[t]
@@ -484,13 +483,16 @@
                 at = slice(k * Z, (k + 1) * Z)
                 value = part[:, at] + pre_ref[g * G + k, y:y + cells].reshape(tall, Z)
                 part_ref[t % 2, k] = value
-                square_ref[t % 2, k] = (value * value).astype(BF)
+                value = value.reshape(cells, C // 8, 8, Z) * inverse
+                value = jnp.sum(value * value, axis=1)
+                square_ref[t % 2, k] = value.reshape(8 * cells, Z).astype(F32)
 
         def second(t):
             a, y = tiles[t]
             square = jnp.concatenate([square_ref[t % 2, k] for k in range(G)], axis=-1)
-            spread = dot(weigh_ref[...], square)
-            spread = lax.rsqrt(spread + norm_eps).reshape(cells, 1, 8, wide)
+            spread = jnp.sum(square.reshape(cells, 8, wide), axis=1, keepdims=True) * (1.0 / C)
+            spread = lax.rsqrt(spread + norm_eps)
+            spread = jnp.broadcast_to(spread, (cells, 8, wide)).reshape(cells, 1, 8, wide)
             for k in range(G):
                 at = slice(k * Z, (k + 1) * Z)
                 value = part_ref[t % 2, k].reshape(cells, C // 8, 8, Z)
@@ -503,12 +505,13 @@
                 first(t)
             if t >= 1:
                 second(t - 1)
-        leave(i, slot).start()
+                leave(i, slot, t - 1).start()
         return carry
 
     lax.fori_loop(0, trips, go, 0)
     for i in range(max(0, trips - 2), trips):
-        leave(i, i % 2).wait()
+        for t in range(len(tiles)):
+            leave(i, i % 2, t).wait()
 
 
 def build(mesh):
@@ -633,9 +636,8 @@
             scratch_shapes=[
                 pltpu.VMEM((2, unroll * G2, yl, C, Z), BF),
                 pltpu.VMEM((2, G2, cells * C, Z), F32),
-                pltpu.VMEM((2, G2, cells * C, Z), BF),
-                pltpu.VMEM((8 * cells, cells * C), BF),
-                pltpu.SemaphoreType.DMA((2,)),
+                pltpu.VMEM((2, G2, 8 * cells, Z), F32),
+                pltpu.SemaphoreType.DMA((2, unroll * yl // cells)),
             ],
             compiler_params=pltpu.CompilerParams(vmem_limit_bytes=12 * 2**20),
             name="back",

time: 41.5 us -> 40.8 us (0.983)
  Pallas kernels: 41.3 us -> 40.6 us
    pallas_call x1, Pallas kernels: 10.2 us -> 9.54 us  [local(): pl.pallas_call(functools.partial(back_kernel, (groups // unroll, G2, yl,...]
where the time goes in v4:
time: 40.8 us; the launch traced here: 40.7 us
  Pallas kernels  40.6 us (100%)
    pallas_call x1, Pallas kernels, local(): pl.pallas_call(functools.partial(front_kernel, sizes), out_shape=(pltpu.V...  31.1 us
    pallas_call x1, Pallas kernels, local(): pl.pallas_call(functools.partial(back_kernel, (groups // unroll, G2, yl,...  9.54 us

profile of v4, /device:TPU:1, one launch (start us, length us, event | category | flops | bytes accessed | tf_op | source)
XLA Modules:
  0.0 40.7 jit_solution(9392074386573383855)
XLA Ops:
  0.0 0.0 copy-start
  0.0 0.0 copy-start.1
  0.0 0.0 copy-start.2
  0.0 31.1 %front.1 = (bf16[8,32,32,128]{3,2,1,0:T(8,128)(2,1)S(1)}, f32[32,32,32,128]{3,2,1,0:T(8,128)S(1)}) custom-call(bf16[32,32,32,128]{3,2,1,0:T(8,128)(2,1)} %bitcast.6, bf16[4,4,2,16,16,32]{5,4,3,2,1,0:T(8,128)(2,1)} %bitcast.7, bf16[1024,256]{1,0:T(8,128)(2,1)} %constant.19.depth_hbm, bf16[4,32,32]{2,1,0:T(8,128)(2,1)} %constant.20.tyf_hbm, ...), custom_call_target="tpu_custom_call" | custom-call | tf_op jit(solution)/shard_map/front/pallas_call | solution.py:569
  31.1 0.0 copy-done
  31.1 0.0 copy-done.1
  31.1 0.0 copy-done.2
  31.2 9.5 %back.1 = bf16[32,32,32,128]{3,2,1,0:T(8,128)(2,1)} custom-call(bf16[8,32,32,128]{3,2,1,0:T(8,128)(2,1)S(1)} %get-tuple-element.7.rows_ref, f32[32,32,32,128]{3,2,1,0:T(8,128)S(1)} %get-tuple-element.8.pre_ref, bf16[128,512]{1,0:T(8,128)(2,1)S(1)} %copy-done, f32[1,32]{1,0:T(1,128)S(1)} %copy-done.1, f32[1,32]{1,0:T(1,128)S(1)} %copy-done.2), custom_call_target="tpu_custom_call" | custom-call | tf_op jit(solution)/shard_map/back/pallas_call | solution.py:631
Async XLA Ops:
  0.0 31.1 %copy-start = (bf16[128,512]{1,0:T(8,128)(2,1)S(1)}, bf16[128,512]{1,0:T(8,128)(2,1)}, u32[]{:S(2)}) copy-start(bf16[128,512]{1,0:T(8,128)(2,1)} %constant.24.depth_ref) | copy-start | bytes 393220
  0.0 31.1 %copy-start.1 = (f32[1,32]{1,0:T(1,128)S(1)}, f32[1,32]{1,0:T(1,128)}, u32[]{:S(2)}) copy-start(f32[1,32]{1,0:T(1,128)} %gain_ref.1) | copy-start | bytes 388
  0.0 31.1 %copy-start.2 = (f32[1,32]{1,0:T(1,128)S(1)}, f32[1,32]{1,0:T(1,128)}, u32[]{:S(2)}) copy-start(f32[1,32]{1,0:T(1,128)} %shift_ref.1) | copy-start | bytes 388
